TPU v7x, 64 devices: a 2x2x8 block of a 4x4x8 slice. The times are simulated.
64 devices in a mesh: stage: 4 (over x, y), data: 16 (over z, core).
Axes of the slice: x: 2, y: 2, z: 8, core: 2. Of those that a mesh axis runs over, the one named last changes fastest.
The devices are a block of a 4x4x8 slice.
Arguments:
- grad_attn: float32 [64, 4, 512, 512], P(('stage', 'data')), parts along dimension 0
- grad_shared_in: float32 [64, 2, 512, 176], P(('stage', 'data')), parts along dimension 0
- grad_shared_out: float32 [64, 1, 176, 512], P(('stage', 'data')), parts along dimension 0
- grad_expert_in: float32 [64, 16, 512, 176], P(('stage', 'data')), parts along dimension 0
- grad_expert_out: float32 [64, 8, 176, 512], P(('stage', 'data')), parts along dimension 0
- mom_attn: float32 [16, 512, 512], P('stage', 'data'), parts along dimension 0
- mom_shared_in: float32 [8, 512, 176], P('stage', 'data'), parts along dimension 0
- mom_shared_out: float32 [4, 176, 512], P('stage', 'data'), parts along dimension 0
- mom_expert_in: float32 [64, 512, 176], P('stage', 'data'), parts along dimension 0
- mom_expert_out: float32 [32, 176, 512], P('stage', 'data'), parts along dimension 0
- master_attn: float32 [16, 512, 512], P('stage', 'data'), parts along dimension 0
- master_shared_in: float32 [8, 512, 176], P('stage', 'data'), parts along dimension 0
- master_shared_out: float32 [4, 176, 512], P('stage', 'data'), parts along dimension 0
- master_expert_in: float32 [64, 512, 176], P('stage', 'data'), parts along dimension 0
- master_expert_out: float32 [32, 176, 512], P('stage', 'data'), parts along dimension 0
Outputs:
- output 1: float32 [16, 512, 512], P('stage', 'data'), parts along dimension 0
- output 2: float32 [8, 512, 176], P('stage', 'data'), parts along dimension 0
- output 3: float32 [4, 176, 512], P('stage', 'data'), parts along dimension 0
- output 4: float32 [64, 512, 176], P('stage', 'data'), parts along dimension 0
- output 5: float32 [32, 176, 512], P('stage', 'data'), parts along dimension 0
- output 6: float32 [16, 512, 512], P('stage', 'data'), parts along dimension 0
- output 7: float32 [8, 512, 176], P('stage', 'data'), parts along dimension 0
- output 8: float32 [4, 176, 512], P('stage', 'data'), parts along dimension 0
- output 9: float32 [64, 512, 176], P('stage', 'data'), parts along dimension 0
- output 10: float32 [32, 176, 512], P('stage', 'data'), parts along dimension 0
- output 11: bfloat16 [16, 512, 512], P('stage'), parts along dimension 0
- output 12: bfloat16 [8, 512, 176], P('stage'), parts along dimension 0
- output 13: bfloat16 [4, 176, 512], P('stage'), parts along dimension 0
- output 14: bfloat16 [64, 512, 176], P('stage'), parts along dimension 0
- output 15: bfloat16 [32, 176, 512], P('stage'), parts along dimension 0
There are 4 independent parts. A program takes and returns all parts, laid end to end along the dimension named above; each array names one.
All inputs are finite; a program needn't handle non-finite values.
Results may differ from a plain program's by a relative error of at most 0.00510666.
Values are sent between devices in bfloat16 or wider.
A program may use at most 768 MiB of HBM per device.

v0:
```python
import math
import jax
import jax.numpy as jnp
from jax import lax
from jax.sharding import PartitionSpec as P

NS_STEPS = 5
MOMENTUM = 0.95
LEARN_RATE = 0.2
WEIGHT_DECAY = 0.25
NORM_EPS = 1e-7
COEF_A = 3.4445
COEF_B = -4.7750
COEF_C = 2.0315


def orthogonalize(mat_stack):
    is_tall = mat_stack.shape[1] > mat_stack.shape[2]
    iterate = mat_stack
    for iteration in range(NS_STEPS):
        if is_tall:
            gram_mat = jnp.einsum("bri,brj->bij", iterate, iterate, preferred_element_type=jnp.float32)
        else:
            gram_mat = jnp.einsum("bir,bjr->bij", iterate, iterate, preferred_element_type=jnp.float32)
        gram_mat = gram_mat.astype(jnp.bfloat16)
        square = jnp.einsum("bij,bjk->bik", gram_mat, gram_mat, preferred_element_type=jnp.float32)
        poly_mat = (COEF_B * gram_mat.astype(jnp.float32) + COEF_C * square).astype(jnp.bfloat16)
        if is_tall:
            update = jnp.einsum("brj,bij->bri", iterate, poly_mat, preferred_element_type=jnp.float32)
        else:
            update = jnp.einsum("bij,bjr->bir", poly_mat, iterate, preferred_element_type=jnp.float32)
        iterate = (COEF_A * iterate.astype(jnp.float32) + update).astype(jnp.bfloat16)
    return iterate


def solution(mesh):
    group_size = mesh.shape["data"]

    def kind_update(grad_full, mom_rows, master_rows):
        mat_count, num_rows, num_cols = grad_full.shape[1], grad_full.shape[2], grad_full.shape[3]
        local_rows = num_rows // group_size
        grad_rows = lax.psum_scatter(grad_full[0], "data", scatter_dimension=1, tiled=True) / group_size
        new_mom = MOMENTUM * mom_rows + grad_rows
        sq_sum = lax.psum(jnp.sum(new_mom * new_mom, axis=(1, 2), keepdims=True), "data")
        start_mat = (new_mom / (jnp.sqrt(sq_sum) + NORM_EPS)).astype(jnp.bfloat16)
        copies = max(1, group_size // mat_count)
        send_buf = jnp.broadcast_to(start_mat[:, None], (mat_count, copies, local_rows, num_cols))
        send_buf = send_buf.reshape(mat_count * copies, local_rows, num_cols)
        owned_mats = lax.all_to_all(send_buf, "data", 0, 1, tiled=True)
        ortho_mat = orthogonalize(owned_mats)
        if copies == 1:
            ortho_rows = lax.all_to_all(ortho_mat, "data", 1, 0, tiled=True)
        else:
            member = lax.axis_index("data") % copies
            block_width = num_cols // copies
            col_block = lax.dynamic_slice_in_dim(ortho_mat[0], member * block_width, block_width, axis=1)
            pieces = lax.all_to_all(col_block.reshape(group_size, local_rows, block_width), "data", 0, 0, tiled=True)
            pieces = pieces.reshape(mat_count, copies, local_rows, block_width).transpose(0, 2, 1, 3)
            ortho_rows = pieces.reshape(mat_count, local_rows, num_cols)
        step_scale = 0.2 * math.sqrt(max(num_rows, num_cols))
        new_master = master_rows - LEARN_RATE * (step_scale * ortho_rows.astype(jnp.float32) + WEIGHT_DECAY * master_rows)
        param_out = lax.all_gather(new_master.astype(jnp.bfloat16), "data", axis=1, tiled=True)
        return new_mom, new_master, param_out

    def local_step(*arrays):
        num_kinds = len(arrays) // 3
        results = [kind_update(arrays[kind_index], arrays[num_kinds + kind_index], arrays[2 * num_kinds + kind_index]) for kind_index in range(num_kinds)]
        return tuple([triple[0] for triple in results] + [triple[1] for triple in results] + [triple[2] for triple in results])

    grad_spec = P(("stage", "data"), None, None, None)
    row_spec = P("stage", "data", None)
    full_spec = P("stage", None, None)
    in_specs = (grad_spec,) * 5 + (row_spec,) * 10
    out_specs = (row_spec,) * 10 + (full_spec,) * 5
    mapped = jax.shard_map(local_step, mesh=mesh, in_specs=in_specs, out_specs=out_specs, check_vma=False)
    return mapped
```

profile of v0, /device:TPU:21, one launch (start us, length us, event | category | flops | bytes accessed | tf_op | source)
XLA Modules:
  0.0 605.6 jit_solution(11021891661810751960)
XLA Ops:
  7.3 2.1 squeeze.21
  9.5 2.4 copy.128
  12.1 3.2 copy.158
  16.1 8.2 %copy.129 = f32[1,16,512,176]{3,2,1,0:T(8,128)} copy(f32[1,16,512,176]{2,3,1,0:T(8,128)} %param.18) | data formatting | bytes 11534336 | tf_op args[3]
  26.2 91.9 %all-reduce.4.cloned.1.call-done = f32[1,176,512]{2,0,1:T(1,128)} async-done(((f32[1,176,512]{2,0,1:T(1,128)}), f32[1,176,512]{2,0,1:T(1,128)}) %all-reduce.4.cloned.1.call-update) | async-done | bytes 360464
  118.2 1.4 multiply_reduce_fusion.4
  119.6 55.3 %reduce-scatter.7.cloned.1.call-done = f32[2,32,176]{2,1,0:T(8,128)} async-done(((f32[2,512,176]{2,1,0:T(8,128)}), f32[2,32,176]{2,1,0:T(8,128)}) %reduce-scatter.7.cloned.1.call-update) | async-done | bytes 45072 | tf_op jit(solution)/shard_map/reduce_scatter | solution.py:42
  174.8 0.9 multiply_reduce_fusion.3
  175.8 58.3 %reduce-scatter.11.cloned.1.call-done = f32[8,11,512]{2,0,1:T(8,128)} async-done(((f32[8,176,512]{2,0,1:T(8,128)}), f32[8,11,512]{2,0,1:T(8,128)}) %reduce-scatter.11.cloned.1.call-update) | async-done | bytes 180240 | tf_op jit(solution)/shard_map/reduce_scatter | solution.py:42
  234.1 1.1 multiply_reduce_fusion.2
  235.2 59.8 %reduce-scatter.5.cloned.1.call-done = f32[4,32,512]{2,1,0:T(8,128)} async-done(((f32[4,512,512]{2,1,0:T(8,128)}), f32[4,32,512]{2,1,0:T(8,128)}) %reduce-scatter.5.cloned.1.call-update) | async-done | bytes 262160 | tf_op jit(solution)/shard_map/reduce_scatter | solution.py:42
  295.0 1.1 multiply_reduce_fusion.1
  296.0 67.6 %reduce-scatter.9.cloned.1.call-done = f32[16,32,176]{2,1,0:T(8,128)} async-done(((f32[16,512,176]{2,1,0:T(8,128)}), f32[16,32,176]{2,1,0:T(8,128)}) %reduce-scatter.9.cloned.1.call-update) | async-done | bytes 360464 | tf_op jit(solution)/shard_map/reduce_scatter | solution.py:42
  363.7 1.3 multiply_reduce_fusion
  364.9 27.2 %all-reduce.1 = (f32[4,1,1]{0,2,1:T(1,128)S(1)}, f32[2,1,1]{0,2,1:T(1,128)S(1)}, f32[1,1,1]{2,1,0:T(1,128)}, f32[16,1,1]{0,2,1:T(1,128)S(1)}, f32[8,1,1]{0,2,1:T(1,128)S(1)}) all-reduce(f32[4,1,1]{0,2,1:T(1,128)S(1)} %bitcast.228, f32[2,1,1]{0,2,1:T(1,128)S(1)} %bitcast.225, ...), channel_id=1, replica_groups=mesh['stage'=4,'data'=16] {'data'}, use_global_device_ids=true, to_apply=%region_6.7 | all-reduce | flops 31 | bytes 248 | tf_op jit(solution)/shard_map/psum | solution.py:44
  393.0 7.5 %all-to-all-start.8 = ((bf16[16,11,512]{2,1,0:T(8,128)(2,1)}), bf16[16,11,512]{2,1,0:T(8,128)(2,1)S(1)}, u32[]{:S(2)}, u32[]{:S(2)}) async-start(bf16[16,11,512]{2,1,0:T(8,128)(2,1)} %bitcast.30), calls=%async_computation.12 | async-start | bytes 524288 | tf_op jit(solution)/shard_map/all_to_all | solution.py:49
  400.5 11.3 %all-to-all-done.8 = bf16[16,11,512]{2,1,0:T(8,128)(2,1)S(1)} async-done(((bf16[16,11,512]{2,1,0:T(8,128)(2,1)}), bf16[16,11,512]{2,1,0:T(8,128)(2,1)S(1)}, u32[]{:S(2)}, u32[]{:S(2)}) %all-to-all-start.8) | async-done | bytes 180256 | tf_op jit(solution)/shard_map/all_to_all | solution.py:49
  415.4 3.7 all-to-all-start.9
  419.2 7.8 %all-to-all-done.9 = bf16[16,11,256]{2,1,0:T(8,128)(2,1)S(1)} async-done(((bf16[16,11,256]{2,1,0:T(8,128)(2,1)}), bf16[16,11,256]{2,1,0:T(8,128)(2,1)S(1)}, u32[]{:S(2)}, u32[]{:S(2)}) %all-to-all-start.9) | async-done | bytes 90144 | tf_op jit(solution)/shard_map/all_to_all | solution.py:57
  427.0 0.8 broadcast_in_dim.19
  427.9 3.7 all-to-all-start
  433.6 14.9 %all-to-all-done = bf16[16,32,512]{2,1,0:T(8,128)(2,1)S(1)} async-done(((bf16[16,32,512]{2,1,0:T(8,128)(2,1)}), bf16[16,32,512]{2,1,0:T(8,128)(2,1)S(1)}, u32[]{:S(2)}, u32[]{:S(2)}) %all-to-all-start) | async-done | bytes 524320 | tf_op jit(solution)/shard_map/all_to_all | solution.py:49
  450.1 0.7 fusion.11
  455.2 3.7 all-to-all-start.1
  459.0 0.8 divide_convert_fusion
  459.8 8.3 %all-to-all-done.1 = bf16[16,32,128]{2,1,0:T(8,128)(2,1)S(1)} async-done(((bf16[16,32,128]{2,1,0:T(8,128)(2,1)}), bf16[16,32,128]{2,1,0:T(8,128)(2,1)S(1)}, u32[]{:S(2)}, u32[]{:S(2)}) %all-to-all-start.1) | async-done | bytes 131104 | tf_op jit(solution)/shard_map/all_to_all | solution.py:57
  468.1 3.9 all-to-all-start.6
  472.1 0.8 fusion.239
  473.1 10.0 %all-to-all-done.6 = bf16[16,32,176]{2,1,0:T(8,128)(2,1)S(1)} async-done(((bf16[16,32,176]{2,1,0:T(8,128)(2,1)}), bf16[16,32,176]{2,1,0:T(8,128)(2,1)S(1)}, u32[]{:S(2)}, u32[]{:S(2)}) %all-to-all-start.6) | async-done | bytes 180256 | tf_op jit(solution)/shard_map/all_to_all | solution.py:49
  483.8 3.7 all-to-all-start.4
  490.1 9.8 %all-to-all-done.4 = bf16[16,11,512]{2,1,0:T(8,128)(2,1)S(1)} async-done(((bf16[16,11,512]{2,1,0:T(8,128)(2,1)}), bf16[16,11,512]{2,1,0:T(8,128)(2,1)S(1)}, u32[]{:S(2)}, u32[]{:S(2)}) %all-to-all-start.4) | async-done | bytes 180256 | tf_op jit(solution)/shard_map/all_to_all | solution.py:49
  500.6 4.0 all-to-all-start.2
  505.9 2.4 reduce.1
  508.3 1.1 reshape.794
  509.7 7.3 %all-to-all-done.2 = bf16[16,32,176]{2,1,0:T(8,128)(2,1)S(1)} async-done(((bf16[16,32,176]{2,1,0:T(8,128)(2,1)}), bf16[16,32,176]{2,1,0:T(8,128)(2,1)S(1)}, u32[]{:S(2)}, u32[]{:S(2)}) %all-to-all-start.2) | async-done | bytes 180256 | tf_op jit(solution)/shard_map/all_to_all | solution.py:49
  517.0 3.7 all-to-all-start.7
  521.5 8.3 %all-to-all-done.7 = bf16[16,2,2816]{2,1,0:T(2,128)(2,1)S(1)} async-done(((bf16[16,2,2816]{2,1,0:T(2,128)(2,1)}), bf16[16,2,2816]{2,1,0:T(2,128)(2,1)S(1)}, u32[]{:S(2)}, u32[]{:S(2)}) %all-to-all-start.7) | async-done | bytes 180256 | tf_op jit(solution)/shard_map/all_to_all | solution.py:52
  529.8 0.8 reshape.795
  530.7 1.0 fusion.236
  534.6 3.7 all-to-all-start.5
  542.0 3.0 all-to-all-done.5
  545.0 3.8 all-to-all-start.3
  549.8 19.2 %all_gather.17 = bf16[1,176,512]{2,0,1:T(2,128)(2,1)S(1)} all-gather(bf16[1,11,512]{2,0,1:T(2,128)(2,1)S(1)} %get-tuple-element.114), channel_id=1, replica_groups=mesh['stage'=4,'data'=16] {'data'}, dimensions={1}, use_global_device_ids=true | all-gather | bytes 191488 | tf_op jit(solution)/shard_map/all_gather | solution.py:62
  570.8 16.8 %all_gather.16 = bf16[2,512,176]{2,1,0:T(8,128)(2,1)S(1)} all-gather(bf16[2,32,176]{2,1,0:T(8,128)(2,1)S(1)} %get-tuple-element.116), channel_id=1, replica_groups=mesh['stage'=4,'data'=16] {'data'}, dimensions={1}, use_global_device_ids=true | all-gather | bytes 382976 | tf_op jit(solution)/shard_map/all_gather | solution.py:62
  587.5 0.9 copy.143
  588.5 2.9 copy.146
  591.4 6.1 %copy.145 = bf16[16,512,176]{1,2,0:T(8,128)(2,1)} copy(bf16[16,512,176]{2,1,0:T(8,128)(2,1)} %all-gather.6.cloned.1.call-done) | data formatting | bytes 5767168
  597.5 1.3 copy.163
  (152 shorter events, 29.8 us)
Async XLA Ops:
  7.2 4.9 copy-start
  7.2 111.0 %all-reduce.4.cloned.1.call-start = ((), (), s32[]{:S(2)}) async-start(), calls=%async_computation.21 | async-start | bytes 720896
  9.4 165.4 %reduce-scatter.7.cloned.1.call-start = ((), (), s32[]{:S(2)}) async-start(), calls=%async_computation.15 | async-start | bytes 1114112 | tf_op jit(solution)/shard_map/reduce_scatter | solution.py:42
  12.0 222.1 %reduce-scatter.11.cloned.1.call-start = ((), (), s32[]{:S(2)}) async-start(), calls=%async_computation.17 | async-start | bytes 3063808 | tf_op jit(solution)/shard_map/reduce_scatter | solution.py:42
  15.4 279.6 %reduce-scatter.5.cloned.1.call-start = ((), (), s32[]{:S(2)}) async-start(), calls=%async_computation.14 | async-start | bytes 4456448 | tf_op jit(solution)/shard_map/reduce_scatter | solution.py:42
  16.0 347.6 %reduce-scatter.9.cloned.1.call-start = ((), (), s32[]{:S(2)}) async-start(), calls=%async_computation.16 | async-start | bytes 8912896 | tf_op jit(solution)/shard_map/reduce_scatter | solution.py:42
  24.3 0.7 copy-start.17
  24.3 93.8 %copy-start.15 = (f32[1,11,512]{2,0,1:T(1,128)S(1)}, f32[1,11,512]{2,0,1:T(1,128)}, u32[]{:S(2)}) copy-start(f32[1,11,512]{2,0,1:T(1,128)} %param.22) | copy-start | bytes 67588
  24.3 150.5 %copy-start.13 = (f32[2,32,176]{2,1,0:T(8,128)S(1)}, f32[2,32,176]{2,1,0:T(8,128)}, u32[]{:S(2)}) copy-start(f32[2,32,176]{2,1,0:T(8,128)} %param.21) | copy-start | bytes 135172
  24.3 209.7 %copy-start.10 = (f32[8,11,512]{2,0,1:T(8,128)S(1)}, f32[8,11,512]{2,0,1:T(8,128)}, u32[]{:S(2)}) copy-start(f32[8,11,512]{2,0,1:T(8,128)} %param.24) | copy-start | bytes 540676
  24.3 270.6 %copy-start.9 = (f32[4,32,512]{2,1,0:T(8,128)S(1)}, f32[4,32,512]{2,1,0:T(8,128)}, u32[]{:S(2)}) copy-start(f32[4,32,512]{2,1,0:T(8,128)} %param.20) | copy-start | bytes 786436
  24.4 339.3 %copy-start.6 = (f32[16,32,176]{2,1,0:T(8,128)S(1)}, f32[16,32,176]{2,1,0:T(8,128)}, u32[]{:S(2)}) copy-start(f32[16,32,176]{2,1,0:T(8,128)} %param.23) | copy-start | bytes 1081348
  119.6 312.8 %copy-start.12 = (f32[1,11,512]{2,0,1:T(1,128)}, f32[1,11,512]{2,0,1:T(1,128)S(1)}, u32[]{:S(2)}) copy-start(f32[1,11,512]{2,0,1:T(1,128)S(1)} %get-tuple-element.147) | copy-start | bytes 67588
  175.8 297.2 %copy-start.8 = (f32[2,32,176]{2,1,0:T(8,128)}, f32[2,32,176]{2,1,0:T(8,128)S(1)}, u32[]{:S(2)}) copy-start(f32[2,32,176]{2,1,0:T(8,128)S(1)} %get-tuple-element.146) | copy-start | bytes 135172
  235.2 177.5 %copy-start.4 = (f32[8,11,512]{2,0,1:T(8,128)}, f32[8,11,512]{2,0,1:T(8,128)S(1)}, u32[]{:S(2)}) copy-start(f32[8,11,512]{2,0,1:T(8,128)S(1)} %get-tuple-element.149) | copy-start | bytes 540676
  296.0 123.1 %copy-start.3 = (f32[4,32,512]{2,1,0:T(8,128)}, f32[4,32,512]{2,1,0:T(8,128)S(1)}, u32[]{:S(2)}) copy-start(f32[4,32,512]{2,1,0:T(8,128)S(1)} %get-tuple-element.145) | copy-start | bytes 786436
  364.9 94.0 %copy-start.2 = (f32[16,32,176]{2,1,0:T(8,128)}, f32[16,32,176]{2,1,0:T(8,128)S(1)}, u32[]{:S(2)}) copy-start(f32[16,32,176]{2,1,0:T(8,128)S(1)} %get-tuple-element.148) | copy-start | bytes 1081348
  393.0 18.8 %all-to-all-start.8 = ((bf16[16,11,512]{2,1,0:T(8,128)(2,1)}), bf16[16,11,512]{2,1,0:T(8,128)(2,1)S(1)}, u32[]{:S(2)}, u32[]{:S(2)}) async-start(bf16[16,11,512]{2,1,0:T(8,128)(2,1)} %bitcast.30), calls=%async_computation.12 | async-start | bytes 524288 | tf_op jit(solution)/shard_map/all_to_all | solution.py:49
  413.8 19.0 %copy-start.11 = (f32[8,11,512]{2,0,1:T(8,128)S(1)}, f32[8,11,512]{2,0,1:T(8,128)}, u32[]{:S(2)}) copy-start(f32[8,11,512]{2,0,1:T(8,128)} %param.29) | copy-start | bytes 540676
  415.4 11.6 %all-to-all-start.9 = ((bf16[16,11,256]{2,1,0:T(8,128)(2,1)}), bf16[16,11,256]{2,1,0:T(8,128)(2,1)S(1)}, u32[]{:S(2)}, u32[]{:S(2)}) async-start(bf16[16,11,256]{2,1,0:T(8,128)(2,1)} %reshape.786), calls=%async_computation.13 | async-start | bytes 262144 | tf_op jit(solution)/shard_map/all_to_all | solution.py:57
  427.9 20.6 %all-to-all-start = ((bf16[16,32,512]{2,1,0:T(8,128)(2,1)}), bf16[16,32,512]{2,1,0:T(8,128)(2,1)S(1)}, u32[]{:S(2)}, u32[]{:S(2)}) async-start(bf16[16,32,512]{2,1,0:T(8,128)(2,1)} %bitcast.6), calls=%async_computation.4 | async-start | bytes 1048576 | tf_op jit(solution)/shard_map/all_to_all | solution.py:49
  431.6 156.9 %all-gather.8.cloned.1.call-start = ((), (), s32[]{:S(2)}) async-start(), calls=%async_computation.20 | async-start | bytes 1531904 | tf_op jit(solution)/shard_map/all_gather | solution.py:62
  453.8 18.3 %copy-start.7 = (f32[4,32,512]{2,1,0:T(8,128)S(1)}, f32[4,32,512]{2,1,0:T(8,128)}, u32[]{:S(2)}) copy-start(f32[4,32,512]{2,1,0:T(8,128)} %param.25) | copy-start | bytes 786436
  455.2 12.8 %all-to-all-start.1 = ((bf16[16,32,128]{2,1,0:T(8,128)(2,1)}), bf16[16,32,128]{2,1,0:T(8,128)(2,1)S(1)}, u32[]{:S(2)}, u32[]{:S(2)}) async-start(bf16[16,32,128]{2,1,0:T(8,128)(2,1)} %bitcast.8), calls=%async_computation.5 | async-start | bytes 262144 | tf_op jit(solution)/shard_map/all_to_all | solution.py:57
  468.1 15.0 %all-to-all-start.6 = ((bf16[16,32,176]{2,1,0:T(8,128)(2,1)}), bf16[16,32,176]{2,1,0:T(8,128)(2,1)S(1)}, u32[]{:S(2)}, u32[]{:S(2)}) async-start(bf16[16,32,176]{2,1,0:T(8,128)(2,1)} %divide_convert_fusion), calls=%async_computation.10 | async-start | bytes 524288 | tf_op jit(solution)/shard_map/all_to_all | solution.py:49
  472.0 119.4 %all-gather.4.cloned.1.call-start = ((), (), s32[]{:S(2)}) async-start(), calls=%async_computation.18 | async-start | bytes 2228224 | tf_op jit(solution)/shard_map/all_gather | solution.py:62
  483.8 16.1 %all-to-all-start.4 = ((bf16[16,11,512]{2,1,0:T(8,128)(2,1)}), bf16[16,11,512]{2,1,0:T(8,128)(2,1)S(1)}, u32[]{:S(2)}, u32[]{:S(2)}) async-start(bf16[16,11,512]{2,1,0:T(8,128)(2,1)} %reshape.783), calls=%async_computation.8 | async-start | bytes 524288 | tf_op jit(solution)/shard_map/all_to_all | solution.py:49
  500.6 16.4 %all-to-all-start.2 = ((bf16[16,32,176]{2,1,0:T(8,128)(2,1)}), bf16[16,32,176]{2,1,0:T(8,128)(2,1)S(1)}, u32[]{:S(2)}, u32[]{:S(2)}) async-start(bf16[16,32,176]{2,1,0:T(8,128)(2,1)} %bitcast.13), calls=%async_computation.6 | async-start | bytes 524288 | tf_op jit(solution)/shard_map/all_to_all | solution.py:49
  505.9 24.8 %copy-start.5 = (f32[16,32,176]{2,1,0:T(8,128)S(1)}, f32[16,32,176]{2,1,0:T(8,128)}, u32[]{:S(2)}) copy-start(f32[16,32,176]{2,1,0:T(8,128)} %param.28) | copy-start | bytes 1081348
  517.0 12.8 %all-to-all-start.7 = ((bf16[16,2,2816]{2,1,0:T(2,128)(2,1)}), bf16[16,2,2816]{2,1,0:T(2,128)(2,1)S(1)}, u32[]{:S(2)}, u32[]{:S(2)}) async-start(bf16[16,2,2816]{2,1,0:T(2,128)(2,1)} %reshape.794), calls=%async_computation.11 | async-start | bytes 360448 | tf_op jit(solution)/shard_map/all_to_all | solution.py:52
  520.7 70.6 %all-gather.6.cloned.1.call-start = ((), (), s32[]{:S(2)}) async-start(), calls=%async_computation.19 | async-start | bytes 4456448 | tf_op jit(solution)/shard_map/all_gather | solution.py:62
  534.6 10.4 %all-to-all-start.5 = ((bf16[16,2,176]{2,1,0:T(2,128)(2,1)}), bf16[16,2,176]{2,1,0:T(2,128)(2,1)S(1)}, u32[]{:S(2)}, u32[]{:S(2)}) async-start(bf16[16,2,176]{2,1,0:T(2,128)(2,1)} %reshape.792), calls=%async_computation.9 | async-start | bytes 32768 | tf_op jit(solution)/shard_map/all_to_all | solution.py:57
  538.9 10.2 %copy-start.16 = (f32[1,11,512]{2,0,1:T(1,128)S(1)}, f32[1,11,512]{2,0,1:T(1,128)}, u32[]{:S(2)}) copy-start(f32[1,11,512]{2,0,1:T(1,128)} %param.27) | copy-start | bytes 67588
  540.0 30.1 %copy-start.14 = (f32[2,32,176]{2,1,0:T(8,128)S(1)}, f32[2,32,176]{2,1,0:T(8,128)}, u32[]{:S(2)}) copy-start(f32[2,32,176]{2,1,0:T(8,128)} %param.26) | copy-start | bytes 135172
  545.0 24.6 %all-to-all-start.3 = ((bf16[16,2,352]{2,1,0:T(2,128)(2,1)}), bf16[16,2,352]{2,1,0:T(2,128)(2,1)S(1)}, u32[]{:S(2)}, u32[]{:S(2)}) async-start(bf16[16,2,352]{2,1,0:T(2,128)(2,1)} %reshape.790), calls=%async_computation.7 | async-start | bytes 49152 | tf_op jit(solution)/shard_map/all_to_all | solution.py:57
  591.4 6.1 %copy-start.1 = (bf16[4,512,512]{2,1,0:T(8,128)(2,1)S(1)}, bf16[4,512,512]{2,1,0:T(8,128)(2,1)}, u32[]{:S(2)}) copy-start(bf16[4,512,512]{2,1,0:T(8,128)(2,1)} %all-gather.4.cloned.1.call-done) | copy-start | bytes 6291460
Sparse Core Ops, SparseCore 0:
  11.0 107.1 all-reduce.3
  121.1 53.7 reduce-scatter.6
  177.7 56.2 reduce-scatter.10
  236.3 58.6 reduce-scatter.4
  297.1 66.4 reduce-scatter.8
  434.3 36.9 all-gather.7
  475.0 42.8 all-gather.3
  531.9 36.2 all-gather.5
where the time goes:
time: 607 us; the launch traced here: 606 us
  waiting for transfers between devices  415 us (68%)
  blocking collectives  63.1 us (10%)
  starting transfers between devices  41.8 us (7%)
  local copies, waits for them, and re-layouts  38.7 us (6%)
  matrix products  16.9 us (3%)
  between operations  16.3 us (3%)
  other arithmetic  14.1 us (2%)
    reduce_scatter x4, waiting for transfers between devices, kind_update(): lax.psum_scatter(grad_full[0], 'data', scatter_dimension=1, tiled=True)  241 us
    unnamed x9, waiting for transfers between devices  92.9 us
    all_to_all x5, waiting for transfers between devices, kind_update(): owned_mats = lax.all_to_all(send_buf, 'data', 0, 1, tiled=True)  53.3 us
    all_gather x2, blocking collectives, kind_update(): lax.all_gather(new_master.astype(jnp.bfloat16), 'data', axis=1, tiled=True)  35.9 us
    unnamed x53, local copies, waits for them, and re-layouts  31.1 us
    psum x1, blocking collectives, kind_update(): lax.psum(jnp.sum(new_mom * new_mom, axis=(1, 2), keepdims=True), 'data')  27.2 us
    all_to_all x5, starting transfers between devices, kind_update(): owned_mats = lax.all_to_all(send_buf, 'data', 0, 1, tiled=True)  22.8 us
    all_to_all x4, waiting for transfers between devices, kind_update(): lax.all_to_all(col_block.reshape(group_size, local_rows, block_width), 'd...  19.2 us
  transfers between devices with their start and end apart: 18, of which 14 were waited for; matrix products, arithmetic and copies ran while one was open for 9% of the time, Pallas kernels for 0%

commit v1 on v0

v1 whole, which is shorter than its diff:
```python
import functools
import math
import jax
import jax.numpy as jnp
from jax import lax
from jax.experimental import pallas as pl
from jax.experimental.pallas import tpu as pltpu
from jax.sharding import PartitionSpec as P

NS_STEPS = 5
MOMENTUM = 0.95
LEARN_RATE = 0.2
WEIGHT_DECAY = 0.25
NORM_EPS = 1e-7
COEF_A = 3.4445
COEF_B = -4.7750
COEF_C = 2.0315

F32 = jnp.float32
BF16 = jnp.bfloat16
MESH = pl.DeviceIdType.MESH
LANE = 128
NT = (((1,), (1,)), ((), ()))


def round_up(value, step):
    return (value + step - 1) // step * step


def fused_step(n, counts, attn_rows, wide, narrow, *refs):
    c_attn, c_si, c_so, c_ei, c_eo = counts
    c_in, c_out = c_si + c_ei, c_so + c_eo
    nz = n // 2
    hops_far, hops_near = nz // 2, nz - 1 - nz // 2
    tiles = wide // LANE
    in_rows = wide // n
    half_in = in_rows // 2
    rest = narrow - LANE
    out_rows = narrow // n
    out_pad = round_up(out_rows, 16)
    attn_blk = attn_rows * tiles
    small_blk = in_rows + half_in
    small0 = c_attn * attn_blk

    it = iter(refs)
    take = lambda k: [next(it) for _ in range(k)]
    g_attn, g_si, g_so, g_ei, g_eo = take(5)
    m_in = take(5)
    w_in = take(5)
    m_out = take(5)
    w_out = take(5)
    p_attn, p_si, p_so, p_ei, p_eo = take(5)
    (gp, rx0, rxr, ag, mp, wp, nat_m, nat_w, nrm, xtx, rxx, otx, rxo, xb, ab, bb) = take(16)
    (s_load, s_nat, s_d2d, s_rs, r_rs, s_nrm, r_nrm, s_x, r_x, s_o, r_o, s_ag, r_ag, s_agd, r_agd, s_out) = take(16)

    in_w = c_in // 2
    waves = []
    base = 0
    for kind, first, cnt in (("in", 0, in_w), ("in", in_w, c_in - in_w), ("out", c_in, c_out)):
        waves.append(dict(kind=kind, first=first, cnt=cnt, row0=small0 + first * small_blk, blk=small_blk, base=base % n))
        base += cnt
    waves.insert(0, dict(kind="attn", first=0, cnt=c_attn, row0=0, blk=attn_blk, base=base % n))
    n_waves = len(waves)
    for w in waves:
        w["rows"] = w["cnt"] * w["blk"]
        w["half"] = w["rows"] // 2
        w["off"] = w["row0"] // 2
        w["ag_half"] = round_up(w["half"], 16)

    me = lax.axis_index("data")
    z = me // 2
    c = lax.rem(me, 2)
    zmod = lambda v: lax.rem(v + 2 * nz, nz)
    dev = lambda zz, cc: {"data": zz * 2 + cc}
    partner = {"data": z * 2 + (1 - c)}
    others = [lax.rem(me + k, n) for k in range(1, n)]

    def remote(src, dst, ss, rs, where):
        return pltpu.make_async_remote_copy(src_ref=src, dst_ref=dst, send_sem=ss, recv_sem=rs,
                                            device_id=where, device_id_type=MESH)

    barrier = pltpu.get_barrier_semaphore()
    for d in others:
        pl.semaphore_signal(barrier, inc=1, device_id={"data": d}, device_id_type=MESH)

    def nat_copies():
        return [pltpu.make_async_copy(srcs[k], dsts[k], s_nat.at[which, k])
                for which, (srcs, dsts) in enumerate(((m_in, nat_m), (w_in, nat_w))) for k in range(5)]

    def small_pack_in(block):
        zero = jnp.zeros((half_in, LANE // 2 - rest), F32)
        return jnp.concatenate([block[:half_in, LANE:], zero, block[half_in:, LANE:], zero], axis=1)

    def load_and_pack(raw_in, raw_out):
        attn_copies = []
        for m in range(c_attn):
            for t in range(tiles):
                attn_copies.append(pltpu.make_async_copy(
                    g_attn.at[m, :, :, :, pl.ds(LANE * t, LANE)],
                    gp.at[:, :, pl.ds(m * attn_blk + t * attn_rows, attn_rows), :], s_load.at[0]))
        k_cut = in_w - c_si
        loads = [
            pltpu.make_async_copy(g_si, raw_in.at[pl.ds(0, c_si)], s_load.at[1]),
            pltpu.make_async_copy(g_ei.at[pl.ds(0, k_cut)], raw_in.at[pl.ds(c_si, k_cut)], s_load.at[2]),
            pltpu.make_async_copy(g_ei.at[pl.ds(k_cut, c_ei - k_cut)], raw_in.at[pl.ds(in_w, c_ei - k_cut)], s_load.at[3]),
            pltpu.make_async_copy(g_so, raw_out.at[pl.ds(0, c_so)], s_load.at[4]),
            pltpu.make_async_copy(g_eo, raw_out.at[pl.ds(c_so, c_eo)], s_load.at[5]),
        ]
        for cp in attn_copies + loads + nat_copies():
            cp.start()

        def pack_in(j, carry):
            off = pl.multiple_of(small0 + small_blk * j, 8)
            for d in range(n):
                block = raw_in[j, in_rows * d:in_rows * (d + 1), :]
                gp[d // 2, d % 2, pl.ds(off, in_rows), :] = block[:, :LANE]
                gp[d // 2, d % 2, pl.ds(off + in_rows, half_in), :] = small_pack_in(block)
            return carry

        def pack_out(j, carry):
            off = pl.multiple_of(small0 + small_blk * (c_in + j), 8)
            for d in range(n):
                rows = [raw_out[j, out_rows * d:out_rows * (d + 1), LANE * t:LANE * (t + 1)] for t in range(tiles)]
                rows.append(jnp.zeros((small_blk - tiles * out_rows, LANE), F32))
                gp[d // 2, d % 2, pl.ds(off, small_blk), :] = jnp.concatenate(rows, axis=0)
            return carry

        pltpu.make_async_copy(gp.at[:, :, pl.ds(0, small0), :], gp.at[:, :, pl.ds(0, small0), :], s_load.at[0]).wait()
        pl.semaphore_wait(barrier, n - 1)
        d2d(0)
        loads[0].wait()
        loads[1].wait()
        lax.fori_loop(0, in_w, pack_in, 0)
        d2d(1)
        loads[2].wait()
        lax.fori_loop(in_w, c_in, pack_in, 0)
        d2d(2)
        loads[3].wait()
        loads[4].wait()
        lax.fori_loop(0, c_out, pack_out, 0)
        d2d(3)

    pending = []

    def d2d_copy(i):
        sl = pl.ds(waves[i]["row0"], waves[i]["rows"])
        return remote(gp.at[:, 1 - c, sl, :], rx0.at[:, sl, :], s_d2d.at[0, i], s_d2d.at[1, i], partner)

    def d2d(i):
        d2d_copy(i).start()

    hops = lambda h, dr: hops_far if h == dr else hops_near
    rs = {}

    def rs_send(i, h, dr, s):
        w = waves[i]
        length = hops(h, dr)
        step = length - s + 1
        dest = zmod(z + step) if dr == 0 else zmod(z - step)
        sl = pl.ds(w["row0"] + h * w["half"], w["half"])
        osl = pl.ds(w["off"], w["half"])
        val = gp[dest, c, sl, :] + rx0[dest, sl, :]
        if s > 1:
            rs[i, h, dr, s - 1].wait_recv()
            val = val + rxr[dr, h, s - 2, osl, :]
        gp[dest, c, sl, :] = val
        where = dev(zmod(z + 1), c) if dr == 0 else dev(zmod(z - 1), c)
        cp = remote(gp.at[dest, c, sl, :], rxr.at[dr, h, s - 1, osl, :],
                    s_rs.at[i, h * 2 + dr, s - 1], r_rs.at[i, h * 2 + dr, s - 1], where)
        cp.start()
        rs[i, h, dr, s] = cp
        pending.append(cp)

    def rs_finish(i):
        w = waves[i]
        for h in range(2):
            sl = pl.ds(w["row0"] + h * w["half"], w["half"])
            osl = pl.ds(w["off"], w["half"])
            total = gp[z, c, sl, :] + rx0[z, sl, :]
            for dr in range(2):
                last = hops(h, dr)
                rs[i, h, dr, last].wait_recv()
                total = total + rxr[dr, h, last - 1, osl, :]
            mp[sl, :] = MOMENTUM * mp[sl, :] + total / n
        lane = lax.broadcasted_iota(jnp.int32, (1, LANE), 1)
        part = jnp.zeros((1, LANE), F32)
        for m in range(w["cnt"]):
            block = mp[pl.ds(w["row0"] + m * w["blk"], w["blk"]), :]
            sq = jnp.sum(jnp.sum(block * block, axis=0, keepdims=True), axis=1, keepdims=True)
            part = jnp.where(lane == m, sq, part)
        nrm[i, me] = part
        for d in others:
            remote(nrm.at[i, me], nrm.at[i, me], s_nrm.at[i], r_nrm.at[i], {"data": d}).start()

    def nrm_wait(i, sem):
        view = nrm.at[i, pl.ds(0, n - 1)]
        pltpu.make_async_copy(view, view, sem).wait()

    def x_copy(i, m):
        w = waves[i]
        owner = (w["base"] + m) % n
        return remote(xtx[i].at[m], rxx[i].at[me], s_x.at[i, m], r_x.at[i], {"data": owner})

    def x_send(i):
        w = waves[i]
        nrm_wait(i, r_nrm.at[i])
        tot = jnp.zeros((1, LANE), F32)
        for d in range(n):
            tot = tot + nrm[i, d]
        lane = lax.broadcasted_iota(jnp.int32, (1, LANE), 1)
        for m in range(w["cnt"]):
            sq = jnp.sum(jnp.where(lane == m, tot, 0.0), axis=1, keepdims=True)
            x = mp[pl.ds(w["row0"] + m * w["blk"], w["blk"]), :] / (jnp.sqrt(sq) + NORM_EPS)
            if w["kind"] == "out":
                zero = jnp.zeros((out_pad - out_rows, LANE), F32)
                parts = []
                for t in range(tiles):
                    parts += [x[t * out_rows:(t + 1) * out_rows], zero]
                x = jnp.concatenate(parts, axis=0)
            x = x.astype(BF16)
            xtx[i][m] = x
            owner = (w["base"] + m) % n

            @pl.when(me != owner)
            def _():
                x_copy(i, m).start()

            @pl.when(me == owner)
            def _():
                rxx[i][me] = x

    def owned(i):
        w = waves[i]
        mine = lax.rem(me - w["base"] + n, n)
        return mine, mine < w["cnt"]

    def assemble(i):
        kind = waves[i]["kind"]
        rx = rxx[i]
        if kind == "attn":
            for t in range(tiles):
                xb[:, LANE * t:LANE * (t + 1)] = rx[:, attn_rows * t:attn_rows * (t + 1), :].reshape(n * attn_rows, LANE)
        elif kind == "out":
            for t in range(tiles):
                xb[:n * out_pad, LANE * t:LANE * (t + 1)] = rx[:, out_pad * t:out_pad * (t + 1), :].reshape(n * out_pad, LANE)
        else:
            hw = n * half_in
            for k in range(2):
                blk = rx[:, half_in * k:half_in * (k + 1), :].reshape(hw, LANE).astype(F32)
                xb[:LANE, hw * k:hw * (k + 1)] = blk.T.astype(BF16)
            blk = rx[:, in_rows:, :].reshape(hw, LANE).astype(F32).T
            for k in range(2):
                xb[LANE:narrow, hw * k:hw * (k + 1)] = blk[k * (LANE // 2):k * (LANE // 2) + rest].astype(BF16)
            xb[narrow:n * out_pad, :] = jnp.zeros((n * out_pad - narrow, wide), BF16)

    def disassemble(i):
        kind = waves[i]["kind"]
        tx = otx[i]
        if kind == "attn":
            for t in range(tiles):
                tx[:, attn_rows * t:attn_rows * (t + 1), :] = xb[:, LANE * t:LANE * (t + 1)].reshape(n, attn_rows, LANE)
        elif kind == "out":
            for t in range(tiles):
                tx[:, out_pad * t:out_pad * (t + 1), :] = xb[:n * out_pad, LANE * t:LANE * (t + 1)].reshape(n, out_pad, LANE)
        else:
            hw = n * half_in
            for k in range(2):
                blk = xb[:LANE, hw * k:hw * (k + 1)].astype(F32).T
                tx[:, half_in * k:half_in * (k + 1), :] = blk.astype(BF16).reshape(n, half_in, LANE)
            zero = jnp.zeros((LANE // 2 - rest, hw), F32)
            parts = []
            for k in range(2):
                parts += [xb[LANE:narrow, hw * k:hw * (k + 1)].astype(F32), zero]
            blk = jnp.concatenate(parts, axis=0).T
            tx[:, in_rows:, :] = blk.astype(BF16).reshape(n, half_in, LANE)

    def iterate(size):
        cut = min(size, 256)

        def one(_, carry):
            for r in range(size // cut):
                sl = slice(r * cut, (r + 1) * cut)
                gram = lax.dot_general(xb[sl, :], xb[:size, :], NT, preferred_element_type=F32)
                ab[sl, :size] = gram.astype(BF16)
            for r in range(size // cut):
                sl = slice(r * cut, (r + 1) * cut)
                square = jnp.dot(ab[sl, :size], ab[:size, :size], preferred_element_type=F32)
                bb[sl, :size] = (COEF_B * ab[sl, :size].astype(F32) + COEF_C * square).astype(BF16)
            for r in range(wide // 256):
                sl = slice(r * 256, (r + 1) * 256)
                update = jnp.dot(bb[:size, :size], xb[:size, sl], preferred_element_type=F32)
                xb[:size, sl] = (COEF_A * xb[:size, sl].astype(F32) + update).astype(BF16)
            return carry

        lax.fori_loop(0, NS_STEPS, one, 0)

    def o_copy(i, mine, d):
        return remote(otx[i].at[d], rxo[i].at[mine], s_o.at[i], r_o.at[i], {"data": d})

    def owner_work(i):
        mine, yes = owned(i)

        @pl.when(yes)
        def _():
            view = rxx[i].at[pl.ds(0, n - 1)]
            pltpu.make_async_copy(view, view, r_x.at[i]).wait()
            assemble(i)
            iterate(n * attn_rows if waves[i]["kind"] == "attn" else n * out_pad)
            disassemble(i)
            for d in others:
                o_copy(i, mine, d).start()
            rxo[i][mine] = otx[i][me]

    def master(i):
        w = waves[i]
        mine, yes = owned(i)
        cnt = w["cnt"]

        @pl.when(yes)
        def _():
            view = rxo[i].at[pl.ds(0, cnt - 1)]
            pltpu.make_async_copy(view, view, r_o.at[i]).wait()

        @pl.when(jnp.logical_not(yes))
        def _():
            pltpu.make_async_copy(rxo[i], rxo[i], r_o.at[i]).wait()

        step_scale = 0.2 * math.sqrt(wide)
        for m in range(cnt):
            sl = pl.ds(w["row0"] + m * w["blk"], w["blk"])
            o = rxo[i][m].astype(F32)
            if w["kind"] == "out":
                parts = [o[out_pad * t:out_pad * t + out_rows] for t in range(tiles)]
                parts.append(jnp.zeros((small_blk - tiles * out_rows, LANE), F32))
                o = jnp.concatenate(parts, axis=0)
            old = wp[sl, :]
            new = old - LEARN_RATE * (step_scale * o + WEIGHT_DECAY * old)
            wp[sl, :] = new
            ag[z, c, sl, :] = new.astype(BF16)

    agc = {}
    agd = {}

    def ag_rows(i, h):
        w = waves[i]
        if h == 0:
            return pl.ds(w["row0"], w["ag_half"])
        return pl.ds(w["row0"] + w["ag_half"], w["rows"] - w["ag_half"])

    def ag_to_partner(i, h, src, key):
        part = ag.at[src, c, ag_rows(i, h), :]
        cp = remote(part, part, s_agd.at[i, h, key], r_agd.at[i, h, key], partner)
        cp.start()
        agd[i, h, key] = cp
        pending.append(cp)

    def ag_send(i, h, dr, s):
        length = hops(h, dr)
        src = z if s == 1 else (zmod(z - (s - 1)) if dr == 0 else zmod(z + (s - 1)))
        if s > 1:
            agc[i, h, dr, s - 1].wait_recv()
        if s <= length:
            part = ag.at[src, c, ag_rows(i, h), :]
            where = dev(zmod(z + 1), c) if dr == 0 else dev(zmod(z - 1), c)
            cp = remote(part, part, s_ag.at[i, h * 2 + dr, s - 1], r_ag.at[i, h * 2 + dr, s - 1], where)
            cp.start()
            agc[i, h, dr, s] = cp
            pending.append(cp)
        if s > 1:
            ag_to_partner(i, h, src, (s - 1) if dr == 0 else nz - (s - 1))
        elif dr == 0:
            ag_to_partner(i, h, src, 0)

    out_copies = []

    def out_copy(src, dst, k):
        cp = pltpu.make_async_copy(src, dst, s_out.at[k])
        cp.start()
        out_copies.append(cp)

    def native_outputs():
        for which, (src, nat, outs) in enumerate(((mp, nat_m, m_out), (wp, nat_w, w_out))):
            for m in range(c_attn):
                for t in range(tiles):
                    nat[0][m, :, LANE * t:LANE * (t + 1)] = src[pl.ds(m * attn_blk + t * attn_rows, attn_rows), :]
            j = 0
            for k, cnt in ((1, c_si), (3, c_ei)):
                for m in range(cnt):
                    off = small0 + small_blk * j
                    nat[k][m, :, :LANE] = src[off:off + in_rows, :]
                    rem_blk = src[off + in_rows:off + small_blk, :]
                    nat[k][m, :half_in, LANE:] = rem_blk[:, :rest]
                    nat[k][m, half_in:, LANE:] = rem_blk[:, LANE // 2:LANE // 2 + rest]
                    j += 1
            for k, cnt in ((2, c_so), (4, c_eo)):
                for m in range(cnt):
                    off = small0 + small_blk * j
                    for t in range(tiles):
                        nat[k][m, :, LANE * t:LANE * (t + 1)] = src[off + t * out_rows:off + (t + 1) * out_rows, :]
                    j += 1
            for k in range(5):
                out_copy(nat[k], outs[k], which * 5 + k)

    def native_inputs():
        for cp in nat_copies():
            cp.wait()
        for nat, dst in ((nat_m, mp), (nat_w, wp)):
            for m in range(c_attn):
                for t in range(tiles):
                    dst[pl.ds(m * attn_blk + t * attn_rows, attn_rows), :] = nat[0][m, :, LANE * t:LANE * (t + 1)]
            j = 0
            for k, cnt in ((1, c_si), (3, c_ei)):
                for m in range(cnt):
                    off = small0 + small_blk * j
                    block = nat[k][m]
                    dst[off:off + in_rows, :] = block[:, :LANE]
                    dst[off + in_rows:off + small_blk, :] = small_pack_in(block)
                    j += 1
            for k, cnt in ((2, c_so), (4, c_eo)):
                for m in range(cnt):
                    off = small0 + small_blk * j
                    rows = [nat[k][m, :, LANE * t:LANE * (t + 1)] for t in range(tiles)]
                    rows.append(jnp.zeros((small_blk - tiles * out_rows, LANE), F32))
                    dst[off:off + small_blk, :] = jnp.concatenate(rows, axis=0)
                    j += 1

    def unpack(i, stage_in, stage_out, flat):
        w = waves[i]
        for h in range(2):
            for key in range(nz):
                agd[i, h, key].wait_recv()
        if w["kind"] == "attn":
            for m in range(c_attn):
                for t in range(tiles):
                    out_copies.append(pltpu.make_async_copy(
                        ag.at[:, :, pl.ds(m * attn_blk + t * attn_rows, attn_rows), :],
                        p_attn.at[m, :, :, :, pl.ds(LANE * t, LANE)], s_out.at[10 + m * tiles + t]))
                    out_copies[-1].start()
        elif w["kind"] == "in":
            def body(j, carry):
                off = pl.multiple_of(small0 + small_blk * j, 16)
                for d in range(n):
                    blk = ag[d // 2, d % 2, pl.ds(off, small_blk), :]
                    r = in_rows * d
                    stage_in[j, r:r + in_rows, :LANE] = blk[:in_rows]
                    tail = blk[in_rows:].astype(F32)
                    stage_in[j, r:r + half_in, LANE:] = tail[:, :rest].astype(BF16)
                    stage_in[j, r + half_in:r + in_rows, LANE:] = tail[:, LANE // 2:LANE // 2 + rest].astype(BF16)
                return carry
            lax.fori_loop(w["first"], w["first"] + w["cnt"], body, 0)
            k = 10 + c_attn * tiles
            if w["first"] == 0:
                out_copy(stage_in.at[pl.ds(0, c_si)], p_si, k)
                out_copy(stage_in.at[pl.ds(c_si, in_w - c_si)], p_ei.at[pl.ds(0, in_w - c_si)], k + 1)
            else:
                out_copy(stage_in.at[pl.ds(in_w, c_in - in_w)], p_ei.at[pl.ds(in_w - c_si, c_in - in_w)], k + 2)
        else:
            def body(j, carry):
                off = pl.multiple_of(small0 + small_blk * (c_in + j), 16)
                for d in range(n):
                    blk = ag[d // 2, d % 2, pl.ds(off, small_blk), :].astype(F32)
                    for t in range(tiles):
                        flat[out_rows * d:out_rows * (d + 1), LANE * t:LANE * (t + 1)] = blk[t * out_rows:(t + 1) * out_rows]
                stage_out[j] = flat[...].astype(BF16)
                return carry
            lax.fori_loop(0, c_out, body, 0)
            k = 13 + c_attn * tiles
            out_copy(stage_out.at[pl.ds(0, c_so)], p_so, k)
            out_copy(stage_out.at[pl.ds(c_so, c_eo)], p_eo, k + 1)

    pl.run_scoped(load_and_pack, pltpu.VMEM((c_in, wide, narrow), F32), pltpu.VMEM((c_out, narrow, wide), F32))
    def main_phase(stage_in, stage_out, flat):
        native_inputs()
        order = range(n_waves)
        for i in order:
            d2d_copy(i).wait_recv()
            for h in range(2):
                for dr in range(2):
                    rs_send(i, h, dr, 1)
        for s in range(2, hops_far + 1):
            for i in order:
                for h in range(2):
                    for dr in range(2):
                        if s <= hops(h, dr):
                            rs_send(i, h, dr, s)
        for i in order:
            rs_finish(i)
        for i in order:
            x_send(i)
        for i in order:
            owner_work(i)
        for i in order:
            master(i)
            for h in range(2):
                for dr in range(2):
                    ag_send(i, h, dr, 1)
        native_outputs()
        for s in range(2, hops_far + 2):
            for i in order:
                for h in range(2):
                    for dr in range(2):
                        if s <= hops(h, dr) + 1:
                            ag_send(i, h, dr, s)

        for i in order:
            unpack(i, stage_in, stage_out, flat)
        for cp in out_copies:
            cp.wait()

        for cp in pending:
            cp.wait_send()
        for i in order:
            d2d_copy(i).wait_send()
            nrm_wait(i, s_nrm.at[i])
            for m in range(waves[i]["cnt"]):
                owner = (waves[i]["base"] + m) % n

                @pl.when(me != owner)
                def _():
                    x_copy(i, m).wait_send()
            mine, yes = owned(i)

            @pl.when(yes)
            def _():
                view = otx[i].at[pl.ds(0, n - 1)]
                pltpu.make_async_copy(view, view, s_o.at[i]).wait()

    pl.run_scoped(main_phase, pltpu.VMEM((c_in, wide, narrow), BF16), pltpu.VMEM((c_out, narrow, wide), BF16),
                  pltpu.VMEM((narrow, wide), F32))


def solution(mesh):
    n = mesh.shape["data"]
    nz = n // 2

    def local_step(*arrays):
        grads, moms, masters = arrays[:5], arrays[5:10], arrays[10:]
        counts = tuple(m.shape[0] for m in moms)
        attn_rows, wide = moms[0].shape[1:]
        narrow = moms[1].shape[2]
        c_attn, c_si, c_so, c_ei, c_eo = counts
        c_in, c_out = c_si + c_ei, c_so + c_eo
        tiles = wide // LANE
        small_blk = wide // n + wide // n // 2
        out_pad = round_up(narrow // n, 16)
        attn_blk = attn_rows * tiles
        rows = c_attn * attn_blk + (c_in + c_out) * small_blk
        grads = [g[0] for g in grads]
        grads[0] = grads[0].reshape(c_attn, nz, 2, attn_rows, wide)
        hops = nz // 2

        sds = jax.ShapeDtypeStruct
        out_shape = [sds(m.shape, F32) for m in moms] * 2
        out_shape += [sds((c_attn, nz, 2, attn_rows, wide), BF16)]
        out_shape += [sds((c_si, wide, narrow), BF16), sds((c_so, narrow, wide), BF16),
                      sds((c_ei, wide, narrow), BF16), sds((c_eo, narrow, wide), BF16)]
        w_cnt = (c_attn, c_in // 2, c_in - c_in // 2, c_out)
        w_blk = (attn_blk, small_blk, small_blk, out_pad * tiles)
        dma = lambda *shape: pltpu.SemaphoreType.DMA(shape)
        vm = pltpu.VMEM
        scratch = [
            vm((nz, 2, rows, LANE), F32),
            vm((nz, rows, LANE), F32),
            vm((2, 2, hops, rows // 2, LANE), F32),
            vm((nz, 2, rows, LANE), BF16),
            vm((rows, LANE), F32),
            vm((rows, LANE), F32),
            [vm(m.shape, F32) for m in moms],
            [vm(m.shape, F32) for m in moms],
            vm((4, n, 1, LANE), F32),
            [vm((k, b, LANE), BF16) for k, b in zip(w_cnt, w_blk)],
            [vm((n, b, LANE), BF16) for b in w_blk],
            [vm((n, b, LANE), BF16) for b in w_blk],
            [vm((k, b, LANE), BF16) for k, b in zip(w_cnt, w_blk)],
            vm((n * attn_rows, wide), BF16),
            vm((n * attn_rows, n * attn_rows), BF16),
            vm((n * attn_rows, n * attn_rows), BF16),
            dma(6), dma(2, 5), dma(2, 4), dma(4, 4, hops), dma(4, 4, hops),
            dma(4), dma(4), dma(4, max(w_cnt)), dma(4), dma(4), dma(4),
            dma(4, 4, hops), dma(4, 4, hops), dma(4, 2, nz), dma(4, 2, nz),
            dma(15 + c_attn * tiles),
        ]
        any_spec = pl.BlockSpec(memory_space=pl.ANY)
        call = pl.pallas_call(
            functools.partial(fused_step, n, counts, attn_rows, wide, narrow),
            out_shape=out_shape,
            in_specs=[any_spec] * 15,
            out_specs=[any_spec] * 15,
            scratch_shapes=scratch,
            compiler_params=pltpu.CompilerParams(
                collective_id=0, has_side_effects=True, vmem_limit_bytes=67043328),
            name="muon_step",
        )
        outs = list(call(*grads, *moms, *masters))
        outs[10] = outs[10].reshape(c_attn, n * attn_rows, wide)
        return tuple(outs)

    grad_spec = P(("stage", "data"), None, None, None)
    row_spec = P("stage", "data", None)
    full_spec = P("stage", None, None)
    in_specs = (grad_spec,) * 5 + (row_spec,) * 10
    out_specs = (row_spec,) * 10 + (full_spec,) * 5
    return jax.shard_map(local_step, mesh=mesh, in_specs=in_specs, out_specs=out_specs, check_vma=False)
```

time: 607 us -> 203 us (0.33)
  waiting for transfers between devices: 415 us -> 0 us
  Pallas kernels: 0 us -> 162 us
  blocking collectives: 63.1 us -> 0 us
  starting transfers between devices: 41.8 us -> 0 us
  matrix products: 16.9 us -> 0 us
  between operations: 16.3 us -> 0.69 us
  other arithmetic: 14.1 us -> 0 us
    reduce_scatter x4 -> x0, waiting for transfers between devices: 241 us -> none  [kind_update(): lax.psum_scatter(grad_full[0], 'data', scatter_dimension=1, tiled=True)]
    pallas_call x0 -> x1, Pallas kernels: none -> 162 us  [local_step(): outs = list(call(*grads, *moms, *masters))]
    unnamed x9 -> x0, waiting for transfers between devices: 92.9 us -> none
    all_to_all x10 -> x0, waiting for transfers between devices: 80.8 us -> none  [the longest x5 53.3 us: kind_update(): owned_mats = lax.all_to_all(send_buf, 'data', 0, 1, tiled=True)]
    all_to_all x10 -> x0, starting transfers between devices: 41.3 us -> none  [the longest x5 22.8 us: kind_update(): owned_mats = lax.all_to_all(send_buf, 'data', 0, 1, tiled=True)]
    all_gather x2 -> x0, blocking collectives: 35.9 us -> none  [kind_update(): lax.all_gather(new_master.astype(jnp.bfloat16), 'data', axis=1, tiled=True)]
    psum x1 -> x0, blocking collectives: 27.2 us -> none  [kind_update(): lax.psum(jnp.sum(new_mom * new_mom, axis=(1, 2), keepdims=True), 'data')]
    dot_general x50 -> x0, matrix products: 16.9 us -> none  [the longest x15 6.98 us: orthogonalize(): jnp.einsum('bij,bjr->bir', poly_mat, iterate, preferred_element_type=jnp....]
  transfers between devices with their start and end apart: 18 -> 0, of which waited for: 14 -> 0; matrix products, arithmetic and copies ran while one was open for 9% -> 0% of each run, Pallas kernels for 0% -> 0%
where the time goes in v1:
time: 203 us; the launch traced here: 201 us
  Pallas kernels  162 us (80%)
  local copies, waits for them, and re-layouts  38.4 us (19%)
    pallas_call x1, Pallas kernels, local_step(): outs = list(call(*grads, *moms, *masters))  162 us
    unnamed x39, local copies, waits for them, and re-layouts  38.4 us

profile of v1, /device:TPU:21, one launch (start us, length us, event | category | flops | bytes accessed | tf_op | source)
XLA Modules:
  0.0 201.0 jit_solution(1629922526682808972)
XLA Ops:
  0.6 1.4 copy.32.refs_7_
  2.0 1.3 copy.34.refs_12_
  3.3 1.7 copy.33.refs_9_
  5.1 1.7 copy.35.refs_14_
  6.8 2.4 %copy.30 = f32[1,2,512,176]{3,2,1,0:T(8,128)} copy(f32[1,2,512,176]{2,3,1,0:T(8,128)} %param.16) | data formatting | bytes 1441792 | tf_op args[1]
  9.2 8.2 %copy.31 = f32[1,16,512,176]{3,2,1,0:T(8,128)} copy(f32[1,16,512,176]{2,3,1,0:T(8,128)} %param.18) | data formatting | bytes 11534336 | tf_op args[3]
  17.4 161.9 %muon_step.1 = (f32[4,32,512]{2,1,0:T(8,128)}, f32[2,32,176]{2,1,0:T(8,128)}, f32[1,11,512]{2,1,0:T(8,128)}, f32[16,32,176]{2,1,0:T(8,128)}, f32[8,11,512]{2,1,0...) custom-call(f32[4,8,2,32,512]{4,3,2,1,0:T(8,128)} %bitcast.8, ...), custom_call_target="tpu_custom_call" | custom-call | tf_op jit(solution)/shard_map/muon_step/pallas_call | solution.py:594
  179.3 1.4 copy.36
  180.7 1.4 copy.38
  182.1 1.7 copy.37
  183.8 1.7 copy.39
  185.5 2.0 copy.40
  187.5 0.0 copy-start.5
  187.5 0.0 copy-start.8
  187.5 0.0 copy-start.3
  187.5 0.0 copy-start.4
  187.5 0.0 copy-start.7
  187.5 0.0 copy-start.2
  187.5 6.1 %copy.41 = bf16[16,512,176]{1,2,0:T(8,128)(2,1)} copy(bf16[16,512,176]{2,1,0:T(8,128)(2,1)} %get-tuple-element.58) | data formatting | bytes 5767168
  193.6 0.0 copy-done.5
  193.6 0.0 copy-start
  193.6 0.7 copy.51
  194.3 0.0 copy-done.8
  194.3 0.6 copy.52
  194.9 0.0 copy-done.3
  194.9 0.8 copy.53
  195.7 0.0 copy-done.4
  195.7 0.0 copy-start.6
  195.7 0.7 copy.54
  196.4 0.0 copy-done.7
  196.4 0.0 copy-start.1
  196.4 0.6 copy.55
  197.1 0.0 copy-done.2
  197.1 0.8 copy.56
  197.9 0.0 copy-done
  197.9 1.3 copy.57
  199.2 0.0 copy-done.6
  199.2 0.7 copy.58
  199.9 0.0 copy-done.1
  199.9 1.1 copy.59
Async XLA Ops:
  187.5 6.1 %copy-start.5 = (f32[4,32,512]{2,1,0:T(8,128)S(1)}, f32[4,32,512]{2,1,0:T(8,128)}, u32[]{:S(2)}) copy-start(f32[4,32,512]{2,1,0:T(8,128)} %get-tuple-element.75) | copy-start | bytes 786436
  187.5 6.8 %copy-start.8 = (f32[2,32,176]{2,1,0:T(8,128)S(1)}, f32[2,32,176]{2,1,0:T(8,128)}, u32[]{:S(2)}) copy-start(f32[2,32,176]{2,1,0:T(8,128)} %get-tuple-element.76) | copy-start | bytes 135172
  187.5 7.4 %copy-start.3 = (f32[16,32,176]{2,1,0:T(8,128)S(1)}, f32[16,32,176]{2,1,0:T(8,128)}, u32[]{:S(2)}) copy-start(f32[16,32,176]{2,1,0:T(8,128)} %get-tuple-element.78) | copy-start | bytes 1081348
  187.5 8.2 %copy-start.4 = (f32[4,32,512]{2,1,0:T(8,128)S(1)}, f32[4,32,512]{2,1,0:T(8,128)}, u32[]{:S(2)}) copy-start(f32[4,32,512]{2,1,0:T(8,128)} %get-tuple-element.80) | copy-start | bytes 786436
  187.5 8.9 %copy-start.7 = (f32[2,32,176]{2,1,0:T(8,128)S(1)}, f32[2,32,176]{2,1,0:T(8,128)}, u32[]{:S(2)}) copy-start(f32[2,32,176]{2,1,0:T(8,128)} %get-tuple-element.81) | copy-start | bytes 135172
  187.5 9.5 %copy-start.2 = (f32[16,32,176]{2,1,0:T(8,128)S(1)}, f32[16,32,176]{2,1,0:T(8,128)}, u32[]{:S(2)}) copy-start(f32[16,32,176]{2,1,0:T(8,128)} %get-tuple-element.83) | copy-start | bytes 1081348
  193.6 4.3 %copy-start = (bf16[4,8,2,32,512]{4,3,2,1,0:T(8,128)(2,1)S(1)}, bf16[4,8,2,32,512]{4,3,2,1,0:T(8,128)(2,1)}, u32[]{:S(2)}) copy-start(bf16[4,8,2,32,512]{4,3,2,1,0:T(8,128)(2,1)} %get-tuple-element.40) | copy-start | bytes 6291460
  195.7 3.5 %copy-start.6 = (bf16[1,176,512]{2,1,0:T(8,128)(2,1)S(1)}, bf16[1,176,512]{2,1,0:T(8,128)(2,1)}, u32[]{:S(2)}) copy-start(bf16[1,176,512]{2,1,0:T(8,128)(2,1)} %get-tuple-element.87) | copy-start | bytes 540676
  196.4 3.4 %copy-start.1 = (bf16[8,176,512]{2,1,0:T(8,128)(2,1)S(1)}, bf16[8,176,512]{2,1,0:T(8,128)(2,1)}, u32[]{:S(2)}) copy-start(bf16[8,176,512]{2,1,0:T(8,128)(2,1)} %get-tuple-element.89) | copy-start | bytes 4325380

commit v2 on v1

--- a/solution.py
+++ b/solution.py
@@ -34,12 +34,12 @@
     hops_far, hops_near = nz // 2, nz - 1 - nz // 2
     tiles = wide // LANE
     in_rows = wide // n
-    half_in = in_rows // 2
-    rest = narrow - LANE
+    groups = LANE // in_rows
     out_rows = narrow // n
     out_pad = round_up(out_rows, 16)
     attn_blk = attn_rows * tiles
-    small_blk = in_rows + half_in
+    small_blk = round_up(tiles * out_rows, 16)
+    cuts = [(q * small_blk, min(small_blk, narrow - q * small_blk)) for q in range(groups)]
     small0 = c_attn * attn_blk
 
     it = iter(refs)
@@ -87,9 +87,25 @@
         return [pltpu.make_async_copy(srcs[k], dsts[k], s_nat.at[which, k])
                 for which, (srcs, dsts) in enumerate(((m_in, nat_m), (w_in, nat_w))) for k in range(5)]
 
-    def small_pack_in(block):
-        zero = jnp.zeros((half_in, LANE // 2 - rest), F32)
-        return jnp.concatenate([block[:half_in, LANE:], zero, block[half_in:, LANE:], zero], axis=1)
+    def lane_swap(blocks):
+        lane = lax.broadcasted_iota(jnp.int32, (1, LANE), 1)
+        blocks = list(blocks)
+        dist = groups // 2
+        while dist:
+            width = dist * in_rows
+            low = lax.rem(lane // width, 2) == 0
+            for q in range(groups):
+                if (q // dist) % 2 == 0:
+                    x, y = blocks[q], blocks[q + dist]
+                    blocks[q] = jnp.where(low, x, pltpu.roll(y, width, axis=1))
+                    blocks[q + dist] = jnp.where(low, pltpu.roll(x, LANE - width, axis=1), y)
+            dist //= 2
+        return blocks
+
+    def pad_rows(x, rows):
+        if x.shape[0] == rows:
+            return x
+        return jnp.concatenate([x, jnp.zeros((rows - x.shape[0], x.shape[1]), x.dtype)], axis=0)
 
     def load_and_pack(raw_in, raw_out):
         attn_copies = []
@@ -111,10 +127,12 @@
 
         def pack_in(j, carry):
             off = pl.multiple_of(small0 + small_blk * j, 8)
-            for d in range(n):
-                block = raw_in[j, in_rows * d:in_rows * (d + 1), :]
-                gp[d // 2, d % 2, pl.ds(off, in_rows), :] = block[:, :LANE]
-                gp[d // 2, d % 2, pl.ds(off + in_rows, half_in), :] = small_pack_in(block)
+            for t in range(tiles):
+                cols = slice(LANE * t, LANE * (t + 1))
+                got = lane_swap([pad_rows(raw_in[j, r:r + k, cols], small_blk) for r, k in cuts])
+                for p in range(groups):
+                    d = groups * t + p
+                    gp[d // 2, d % 2, pl.ds(off, small_blk), :] = got[p]
             return carry
 
         def pack_out(j, carry):
@@ -244,13 +262,10 @@
             for t in range(tiles):
                 xb[:n * out_pad, LANE * t:LANE * (t + 1)] = rx[:, out_pad * t:out_pad * (t + 1), :].reshape(n * out_pad, LANE)
         else:
-            hw = n * half_in
-            for k in range(2):
-                blk = rx[:, half_in * k:half_in * (k + 1), :].reshape(hw, LANE).astype(F32)
-                xb[:LANE, hw * k:hw * (k + 1)] = blk.T.astype(BF16)
-            blk = rx[:, in_rows:, :].reshape(hw, LANE).astype(F32).T
-            for k in range(2):
-                xb[LANE:narrow, hw * k:hw * (k + 1)] = blk[k * (LANE // 2):k * (LANE // 2) + rest].astype(BF16)
+            for t in range(tiles):
+                got = lane_swap([rx[groups * t + p].astype(F32) for p in range(groups)])
+                for q, (r, k) in enumerate(cuts):
+                    xb[r:r + k, LANE * t:LANE * (t + 1)] = got[q][:k].astype(BF16)
             xb[narrow:n * out_pad, :] = jnp.zeros((n * out_pad - narrow, wide), BF16)
 
     def disassemble(i):
@@ -263,16 +278,11 @@
             for t in range(tiles):
                 tx[:, out_pad * t:out_pad * (t + 1), :] = xb[:n * out_pad, LANE * t:LANE * (t + 1)].reshape(n, out_pad, LANE)
         else:
-            hw = n * half_in
-            for k in range(2):
-                blk = xb[:LANE, hw * k:hw * (k + 1)].astype(F32).T
-                tx[:, half_in * k:half_in * (k + 1), :] = blk.astype(BF16).reshape(n, half_in, LANE)
-            zero = jnp.zeros((LANE // 2 - rest, hw), F32)
-            parts = []
-            for k in range(2):
-                parts += [xb[LANE:narrow, hw * k:hw * (k + 1)].astype(F32), zero]
-            blk = jnp.concatenate(parts, axis=0).T
-            tx[:, in_rows:, :] = blk.astype(BF16).reshape(n, half_in, LANE)
+            for t in range(tiles):
+                cols = slice(LANE * t, LANE * (t + 1))
+                got = lane_swap([pad_rows(xb[r:r + k, cols].astype(F32), small_blk) for r, k in cuts])
+                for p in range(groups):
+                    tx[groups * t + p] = got[p].astype(BF16)
 
     def iterate(size):
         cut = min(size, 256)
@@ -385,18 +395,20 @@
                     nat[0][m, :, LANE * t:LANE * (t + 1)] = src[pl.ds(m * attn_blk + t * attn_rows, attn_rows), :]
             j = 0
             for k, cnt in ((1, c_si), (3, c_ei)):
-                for m in range(cnt):
-                    off = small0 + small_blk * j
-                    nat[k][m, :, :LANE] = src[off:off + in_rows, :]
-                    rem_blk = src[off + in_rows:off + small_blk, :]
-                    nat[k][m, :half_in, LANE:] = rem_blk[:, :rest]
-                    nat[k][m, half_in:, LANE:] = rem_blk[:, LANE // 2:LANE // 2 + rest]
-                    j += 1
+                for m in range(0, cnt, groups):
+                    some = min(groups, cnt - m)
+                    off = small0 + small_blk * (j + m)
+                    got = [src[off + small_blk * p:off + small_blk * (p + 1), :] for p in range(some)]
+                    got += [jnp.zeros((small_blk, LANE), F32)] * (groups - some)
+                    block = pad_rows(jnp.concatenate(lane_swap(got), axis=0), 2 * LANE).T
+                    for p in range(some):
+                        nat[k][m + p] = block[in_rows * p:in_rows * (p + 1), :narrow]
+                j += cnt
             for k, cnt in ((2, c_so), (4, c_eo)):
                 for m in range(cnt):
                     off = small0 + small_blk * j
                     for t in range(tiles):
-                        nat[k][m, :, LANE * t:LANE * (t + 1)] = src[off + t * out_rows:off + (t + 1) * out_rows, :]
+                        nat[k][:, m, LANE * t:LANE * (t + 1)] = src[off + t * out_rows:off + (t + 1) * out_rows, :]
                     j += 1
             for k in range(5):
                 out_copy(nat[k], outs[k], which * 5 + k)
@@ -410,18 +422,18 @@
                     dst[pl.ds(m * attn_blk + t * attn_rows, attn_rows), :] = nat[0][m, :, LANE * t:LANE * (t + 1)]
             j = 0
             for k, cnt in ((1, c_si), (3, c_ei)):
-                for m in range(cnt):
-                    off = small0 + small_blk * j
-                    block = nat[k][m]
-                    dst[off:off + in_rows, :] = block[:, :LANE]
-                    dst[off + in_rows:off + small_blk, :] = small_pack_in(block)
-                    j += 1
+                for m in range(0, cnt, groups):
+                    some = min(groups, cnt - m)
+                    block = pad_rows(jnp.concatenate([nat[k][m + p] for p in range(some)], axis=0), LANE)
+                    block = jnp.concatenate([block, jnp.zeros((LANE, 2 * LANE - narrow), F32)], axis=1).T
+                    got = lane_swap([block[small_blk * q:small_blk * (q + 1)] for q in range(groups)])
+                    for p in range(some):
+                        dst[pl.ds(small0 + small_blk * (j + m + p), small_blk), :] = got[p]
+                j += cnt
             for k, cnt in ((2, c_so), (4, c_eo)):
                 for m in range(cnt):
-                    off = small0 + small_blk * j
-                    rows = [nat[k][m, :, LANE * t:LANE * (t + 1)] for t in range(tiles)]
-                    rows.append(jnp.zeros((small_blk - tiles * out_rows, LANE), F32))
-                    dst[off:off + small_blk, :] = jnp.concatenate(rows, axis=0)
+                    rows = [nat[k][:, m, LANE * t:LANE * (t + 1)] for t in range(tiles)]
+                    dst[pl.ds(small0 + small_blk * j, small_blk), :] = pad_rows(jnp.concatenate(rows, axis=0), small_blk)
                     j += 1
 
     def unpack(i, stage_in, stage_out, flat):
@@ -439,13 +451,11 @@
         elif w["kind"] == "in":
             def body(j, carry):
                 off = pl.multiple_of(small0 + small_blk * j, 16)
-                for d in range(n):
-                    blk = ag[d // 2, d % 2, pl.ds(off, small_blk), :]
-                    r = in_rows * d
-                    stage_in[j, r:r + in_rows, :LANE] = blk[:in_rows]
-                    tail = blk[in_rows:].astype(F32)
-                    stage_in[j, r:r + half_in, LANE:] = tail[:, :rest].astype(BF16)
-                    stage_in[j, r + half_in:r + in_rows, LANE:] = tail[:, LANE // 2:LANE // 2 + rest].astype(BF16)
+                for t in range(tiles):
+                    devs = [groups * t + p for p in range(groups)]
+                    got = lane_swap([ag[d // 2, d % 2, pl.ds(off, small_blk), :].astype(F32) for d in devs])
+                    for q, (r, k) in enumerate(cuts):
+                        stage_in[j, r:r + k, LANE * t:LANE * (t + 1)] = got[q][:k].astype(BF16)
                 return carry
             lax.fori_loop(w["first"], w["first"] + w["cnt"], body, 0)
             k = 10 + c_attn * tiles
@@ -468,7 +478,7 @@
             out_copy(stage_out.at[pl.ds(0, c_so)], p_so, k)
             out_copy(stage_out.at[pl.ds(c_so, c_eo)], p_eo, k + 1)
 
-    pl.run_scoped(load_and_pack, pltpu.VMEM((c_in, wide, narrow), F32), pltpu.VMEM((c_out, narrow, wide), F32))
+    pl.run_scoped(load_and_pack, pltpu.VMEM((c_in, narrow, wide), F32), pltpu.VMEM((c_out, narrow, wide), F32))
     def main_phase(stage_in, stage_out, flat):
         native_inputs()
         order = range(n_waves)
@@ -525,8 +535,38 @@
                 view = otx[i].at[pl.ds(0, n - 1)]
                 pltpu.make_async_copy(view, view, s_o.at[i]).wait()
 
-    pl.run_scoped(main_phase, pltpu.VMEM((c_in, wide, narrow), BF16), pltpu.VMEM((c_out, narrow, wide), BF16),
+    pl.run_scoped(main_phase, pltpu.VMEM((c_in, narrow, wide), BF16), pltpu.VMEM((c_out, narrow, wide), BF16),
                   pltpu.VMEM((narrow, wide), F32))
+
+
+def hand_over(shapes):
+    count = len(shapes)
+    pieces = []
+    for k, x in enumerate(shapes):
+        parts = next((p for p in (4, 2) if x.shape[0] % p == 0 and x.size > 400000), 1)
+        step = x.shape[0] // parts
+        pieces += [(k, p * step, step) for p in range(parts)]
+
+    def kernel(*refs):
+        src, dst, buf, sem_in, sem_out = refs[:count], refs[count:2 * count], refs[2 * count:3 * count], refs[-2], refs[-1]
+        first = [pltpu.make_async_copy(src[k].at[pl.ds(r, m)], buf[k].at[pl.ds(r, m)], sem_in.at[i])
+                 for i, (k, r, m) in enumerate(pieces)]
+        second = [pltpu.make_async_copy(buf[k].at[pl.ds(r, m)], dst[k].at[pl.ds(r, m)], sem_out.at[i])
+                  for i, (k, r, m) in enumerate(pieces)]
+        for cp in first:
+            cp.start()
+        for one, two in zip(first, second):
+            one.wait()
+            two.start()
+        for cp in second:
+            cp.wait()
+
+    any_spec = pl.BlockSpec(memory_space=pl.ANY)
+    return pl.pallas_call(
+        kernel, out_shape=shapes, in_specs=[any_spec] * count, out_specs=[any_spec] * count,
+        scratch_shapes=[pltpu.VMEM(x.shape, x.dtype) for x in shapes]
+        + [pltpu.SemaphoreType.DMA((len(pieces),)), pltpu.SemaphoreType.DMA((len(pieces),))],
+        name="hand_over")
 
 
 def solution(mesh):
@@ -541,19 +581,22 @@
         c_attn, c_si, c_so, c_ei, c_eo = counts
         c_in, c_out = c_si + c_ei, c_so + c_eo
         tiles = wide // LANE
-        small_blk = wide // n + wide // n // 2
+        small_blk = round_up(tiles * (narrow // n), 16)
         out_pad = round_up(narrow // n, 16)
         attn_blk = attn_rows * tiles
         rows = c_attn * attn_blk + (c_in + c_out) * small_blk
+        turn = lambda x: jnp.swapaxes(x, -1, -2)
         grads = [g[0] for g in grads]
+        grads[1], grads[3] = turn(grads[1]), turn(grads[3])
+        flip = lambda arrs: [jnp.swapaxes(x, 0, 1) if k in (2, 4) else x for k, x in enumerate(arrs)]
+        moms, masters = flip(moms), flip(masters)
         grads[0] = grads[0].reshape(c_attn, nz, 2, attn_rows, wide)
         hops = nz // 2
 
         sds = jax.ShapeDtypeStruct
         out_shape = [sds(m.shape, F32) for m in moms] * 2
         out_shape += [sds((c_attn, nz, 2, attn_rows, wide), BF16)]
-        out_shape += [sds((c_si, wide, narrow), BF16), sds((c_so, narrow, wide), BF16),
-                      sds((c_ei, wide, narrow), BF16), sds((c_eo, narrow, wide), BF16)]
+        out_shape += [sds((k, narrow, wide), BF16) for k in counts[1:]]
         w_cnt = (c_attn, c_in // 2, c_in - c_in // 2, c_out)
         w_blk = (attn_blk, small_blk, small_blk, out_pad * tiles)
         dma = lambda *shape: pltpu.SemaphoreType.DMA(shape)
@@ -591,8 +634,10 @@
                 collective_id=0, has_side_effects=True, vmem_limit_bytes=67043328),
             name="muon_step",
         )
-        outs = list(call(*grads, *moms, *masters))
+        outs = list(hand_over(out_shape)(*call(*grads, *moms, *masters)))
+        outs[:5], outs[5:10] = flip(outs[:5]), flip(outs[5:10])
         outs[10] = outs[10].reshape(c_attn, n * attn_rows, wide)
+        outs[11], outs[13] = turn(outs[11]), turn(outs[13])
         return tuple(outs)
 
     grad_spec = P(("stage", "data"), None, None, None)

time: 203 us -> 178 us (0.88)
  local copies, waits for them, and re-layouts: 38.4 us -> 0 us
  Pallas kernels: 162 us -> 177 us
    unnamed x39 -> x0, local copies, waits for them, and re-layouts: 38.4 us -> none
    pallas_call x1 -> x2, Pallas kernels: 162 us -> 177 us  [local_step(): outs = list(hand_over(out_shape)(*call(*grads, *moms, *masters)))]
where the time goes in v2:
time: 178 us
  Pallas kernels  177 us (99%)
    pallas_call x2, Pallas kernels, local_step(): outs = list(hand_over(out_shape)(*call(*grads, *moms, *masters)))  177 us

profile of v2, /device:TPU:21, one launch (start us, length us, event | category | flops | bytes accessed | tf_op | source)
XLA Modules:
  0.0 177.6 jit_solution(5999740592589175955)
XLA Ops:
  0.7 169.7 %muon_step.1 = (f32[4,32,512]{2,1,0:T(8,128)}, f32[2,32,176]{2,1,0:T(8,128)}, f32[11,1,512]{2,1,0:T(1,128)}, f32[16,32,176]{2,1,0:T(8,128)}, f32[11,8,512]{2,1,0...) custom-call(f32[4,8,2,32,512]{4,3,2,1,0:T(8,128)} %bitcast.21, ...), custom_call_target="tpu_custom_call" | custom-call | tf_op jit(solution)/shard_map/muon_step/pallas_call | solution.py:637
  170.3 7.1 %hand_over.1 = (f32[4,32,512]{2,1,0:T(8,128)}, f32[2,32,176]{2,1,0:T(8,128)}, f32[11,1,512]{2,1,0:T(1,128)}, f32[16,32,176]{2,1,0:T(8,128)}, f32[11,8,512]{2,1,0...) custom-call(f32[4,32,512]{2,1,0:T(8,128)} %get-tuple-element.45.refs, ...), custom_call_target="tpu_custom_call" | custom-call | tf_op jit(solution)/shard_map/hand_over/pallas_call | solution.py:637

commit v3 on v2

--- a/solution.py
+++ b/solution.py
@@ -50,7 +50,8 @@
     m_out = take(5)
     w_out = take(5)
     p_attn, p_si, p_so, p_ei, p_eo = take(5)
-    (gp, rx0, rxr, ag, mp, wp, nat_m, nat_w, nrm, xtx, rxx, otx, rxo, xb, ab, bb) = take(16)
+    (gp, rx0, rxr, ag, mp, wp, nat_m, nat_w, nrm, xtx, rxx, otx, rxo, xb, ab, bb,
+     raw_in, raw_out, stage_in, stage_out, flat) = take(21)
     (s_load, s_nat, s_d2d, s_rs, r_rs, s_nrm, r_nrm, s_x, r_x, s_o, r_o, s_ag, r_ag, s_agd, r_agd, s_out) = take(16)
 
     in_w = c_in // 2
@@ -107,65 +108,80 @@
             return x
         return jnp.concatenate([x, jnp.zeros((rows - x.shape[0], x.shape[1]), x.dtype)], axis=0)
 
-    def load_and_pack(raw_in, raw_out):
-        attn_copies = []
-        for m in range(c_attn):
-            for t in range(tiles):
-                attn_copies.append(pltpu.make_async_copy(
-                    g_attn.at[m, :, :, :, pl.ds(LANE * t, LANE)],
-                    gp.at[:, :, pl.ds(m * attn_blk + t * attn_rows, attn_rows), :], s_load.at[0]))
-        k_cut = in_w - c_si
-        loads = [
+    k_cut = in_w - c_si
+
+    def loads():
+        return [
             pltpu.make_async_copy(g_si, raw_in.at[pl.ds(0, c_si)], s_load.at[1]),
             pltpu.make_async_copy(g_ei.at[pl.ds(0, k_cut)], raw_in.at[pl.ds(c_si, k_cut)], s_load.at[2]),
             pltpu.make_async_copy(g_ei.at[pl.ds(k_cut, c_ei - k_cut)], raw_in.at[pl.ds(in_w, c_ei - k_cut)], s_load.at[3]),
             pltpu.make_async_copy(g_so, raw_out.at[pl.ds(0, c_so)], s_load.at[4]),
             pltpu.make_async_copy(g_eo, raw_out.at[pl.ds(c_so, c_eo)], s_load.at[5]),
         ]
-        for cp in attn_copies + loads + nat_copies():
+
+    def start_loads():
+        for m in range(c_attn):
+            for t in range(tiles):
+                pltpu.make_async_copy(
+                    g_attn.at[m, :, :, :, pl.ds(LANE * t, LANE)],
+                    gp.at[:, :, pl.ds(m * attn_blk + t * attn_rows, attn_rows), :], s_load.at[0]).start()
+        for cp in loads() + nat_copies():
             cp.start()
 
-        def pack_in(j, carry):
-            off = pl.multiple_of(small0 + small_blk * j, 8)
-            for t in range(tiles):
-                cols = slice(LANE * t, LANE * (t + 1))
-                got = lane_swap([pad_rows(raw_in[j, r:r + k, cols], small_blk) for r, k in cuts])
-                for p in range(groups):
-                    d = groups * t + p
-                    gp[d // 2, d % 2, pl.ds(off, small_blk), :] = got[p]
-            return carry
-
-        def pack_out(j, carry):
-            off = pl.multiple_of(small0 + small_blk * (c_in + j), 8)
-            for d in range(n):
-                rows = [raw_out[j, out_rows * d:out_rows * (d + 1), LANE * t:LANE * (t + 1)] for t in range(tiles)]
-                rows.append(jnp.zeros((small_blk - tiles * out_rows, LANE), F32))
-                gp[d // 2, d % 2, pl.ds(off, small_blk), :] = jnp.concatenate(rows, axis=0)
-            return carry
-
-        pltpu.make_async_copy(gp.at[:, :, pl.ds(0, small0), :], gp.at[:, :, pl.ds(0, small0), :], s_load.at[0]).wait()
-        pl.semaphore_wait(barrier, n - 1)
-        d2d(0)
-        loads[0].wait()
-        loads[1].wait()
-        lax.fori_loop(0, in_w, pack_in, 0)
-        d2d(1)
-        loads[2].wait()
-        lax.fori_loop(in_w, c_in, pack_in, 0)
-        d2d(2)
-        loads[3].wait()
-        loads[4].wait()
-        lax.fori_loop(0, c_out, pack_out, 0)
-        d2d(3)
+    def pack_in(j, carry):
+        off = pl.multiple_of(small0 + small_blk * j, 8)
+        for t in range(tiles):
+            cols = slice(LANE * t, LANE * (t + 1))
+            got = lane_swap([pad_rows(raw_in[j, r:r + k, cols], small_blk) for r, k in cuts])
+            for p in range(groups):
+                d = groups * t + p
+                gp[d // 2, d % 2, pl.ds(off, small_blk), :] = got[p]
+        return carry
+
+    def pack_out(j, carry):
+        off = pl.multiple_of(small0 + small_blk * (c_in + j), 8)
+        for d in range(n):
+            rows = [raw_out[j, out_rows * d:out_rows * (d + 1), LANE * t:LANE * (t + 1)] for t in range(tiles)]
+            gp[d // 2, d % 2, pl.ds(off, small_blk), :] = pad_rows(jnp.concatenate(rows, axis=0), small_blk)
+        return carry
+
+    def pack(i):
+        load = loads()
+        if i == 0:
+            view = gp.at[:, :, pl.ds(0, small0), :]
+            pltpu.make_async_copy(view, view, s_load.at[0]).wait()
+            pl.semaphore_wait(barrier, n - 1)
+        elif i == 1:
+            load[0].wait()
+            load[1].wait()
+            lax.fori_loop(0, in_w, pack_in, 0)
+        elif i == 2:
+            load[2].wait()
+            lax.fori_loop(in_w, c_in, pack_in, 0)
+        else:
+            load[3].wait()
+            load[4].wait()
+            lax.fori_loop(0, c_out, pack_out, 0)
+        for k in near_last:
+            d2d_copy(i, k).start()
 
     pending = []
 
-    def d2d_copy(i):
+    near_last = [hops_far]
+    for k in range(hops_near, 0, -1):
+        near_last += [k, nz - k]
+    near_last.append(0)
+    d2d_seen = set()
+
+    def d2d_copy(i, k):
         sl = pl.ds(waves[i]["row0"], waves[i]["rows"])
-        return remote(gp.at[:, 1 - c, sl, :], rx0.at[:, sl, :], s_d2d.at[0, i], s_d2d.at[1, i], partner)
-
-    def d2d(i):
-        d2d_copy(i).start()
+        dest = zmod(z + k)
+        return remote(gp.at[dest, 1 - c, sl, :], rx0.at[dest, sl, :], s_d2d.at[0, i, k], s_d2d.at[1, i, k], partner)
+
+    def d2d_wait(i, k):
+        if (i, k) not in d2d_seen:
+            d2d_seen.add((i, k))
+            d2d_copy(i, k).wait_recv()
 
     hops = lambda h, dr: hops_far if h == dr else hops_near
     rs = {}
@@ -175,6 +191,7 @@
         length = hops(h, dr)
         step = length - s + 1
         dest = zmod(z + step) if dr == 0 else zmod(z - step)
+        d2d_wait(i, step if dr == 0 else nz - step)
         sl = pl.ds(w["row0"] + h * w["half"], w["half"])
         osl = pl.ds(w["off"], w["half"])
         val = gp[dest, c, sl, :] + rx0[dest, sl, :]
@@ -191,6 +208,7 @@
 
     def rs_finish(i):
         w = waves[i]
+        d2d_wait(i, 0)
         for h in range(2):
             sl = pl.ds(w["row0"] + h * w["half"], w["half"])
             osl = pl.ds(w["off"], w["half"])
@@ -284,7 +302,7 @@
                 for p in range(groups):
                     tx[groups * t + p] = got[p].astype(BF16)
 
-    def iterate(size):
+    def iterate(size, steps):
         cut = min(size, 256)
 
         def one(_, carry):
@@ -302,24 +320,26 @@
                 xb[:size, sl] = (COEF_A * xb[:size, sl].astype(F32) + update).astype(BF16)
             return carry
 
-        lax.fori_loop(0, NS_STEPS, one, 0)
+        lax.fori_loop(0, steps, one, 0)
 
     def o_copy(i, mine, d):
         return remote(otx[i].at[d], rxo[i].at[mine], s_o.at[i], r_o.at[i], {"data": d})
 
-    def owner_work(i):
+    def owner_work(i, begin, steps, end):
         mine, yes = owned(i)
 
         @pl.when(yes)
         def _():
-            view = rxx[i].at[pl.ds(0, n - 1)]
-            pltpu.make_async_copy(view, view, r_x.at[i]).wait()
-            assemble(i)
-            iterate(n * attn_rows if waves[i]["kind"] == "attn" else n * out_pad)
-            disassemble(i)
-            for d in others:
-                o_copy(i, mine, d).start()
-            rxo[i][mine] = otx[i][me]
+            if begin:
+                view = rxx[i].at[pl.ds(0, n - 1)]
+                pltpu.make_async_copy(view, view, r_x.at[i]).wait()
+                assemble(i)
+            iterate(n * attn_rows if waves[i]["kind"] == "attn" else n * out_pad, steps)
+            if end:
+                disassemble(i)
+                for d in others:
+                    o_copy(i, mine, d).start()
+                rxo[i][mine] = otx[i][me]
 
     def master(i):
         w = waves[i]
@@ -388,8 +408,8 @@
         cp.start()
         out_copies.append(cp)
 
-    def native_outputs():
-        for which, (src, nat, outs) in enumerate(((mp, nat_m, m_out), (wp, nat_w, w_out))):
+    def native_outputs(which):
+        for src, nat, outs in (((mp, nat_m, m_out), (wp, nat_w, w_out))[which],):
             for m in range(c_attn):
                 for t in range(tiles):
                     nat[0][m, :, LANE * t:LANE * (t + 1)] = src[pl.ds(m * attn_blk + t * attn_rows, attn_rows), :]
@@ -413,10 +433,10 @@
             for k in range(5):
                 out_copy(nat[k], outs[k], which * 5 + k)
 
-    def native_inputs():
-        for cp in nat_copies():
+    def native_inputs(which):
+        for cp in nat_copies()[5 * which:5 * which + 5]:
             cp.wait()
-        for nat, dst in ((nat_m, mp), (nat_w, wp)):
+        for nat, dst in (((nat_m, mp), (nat_w, wp))[which],):
             for m in range(c_attn):
                 for t in range(tiles):
                     dst[pl.ds(m * attn_blk + t * attn_rows, attn_rows), :] = nat[0][m, :, LANE * t:LANE * (t + 1)]
@@ -436,7 +456,7 @@
                     dst[pl.ds(small0 + small_blk * j, small_blk), :] = pad_rows(jnp.concatenate(rows, axis=0), small_blk)
                     j += 1
 
-    def unpack(i, stage_in, stage_out, flat):
+    def unpack(i):
         w = waves[i]
         for h in range(2):
             for key in range(nz):
@@ -478,65 +498,106 @@
             out_copy(stage_out.at[pl.ds(0, c_so)], p_so, k)
             out_copy(stage_out.at[pl.ds(c_so, c_eo)], p_eo, k + 1)
 
-    pl.run_scoped(load_and_pack, pltpu.VMEM((c_in, narrow, wide), F32), pltpu.VMEM((c_out, narrow, wide), F32))
-    def main_phase(stage_in, stage_out, flat):
-        native_inputs()
-        order = range(n_waves)
-        for i in order:
-            d2d_copy(i).wait_recv()
-            for h in range(2):
-                for dr in range(2):
-                    rs_send(i, h, dr, 1)
-        for s in range(2, hops_far + 1):
-            for i in order:
-                for h in range(2):
-                    for dr in range(2):
-                        if s <= hops(h, dr):
-                            rs_send(i, h, dr, s)
-        for i in order:
-            rs_finish(i)
-        for i in order:
-            x_send(i)
-        for i in order:
-            owner_work(i)
-        for i in order:
-            master(i)
-            for h in range(2):
-                for dr in range(2):
-                    ag_send(i, h, dr, 1)
-        native_outputs()
-        for s in range(2, hops_far + 2):
-            for i in order:
-                for h in range(2):
-                    for dr in range(2):
-                        if s <= hops(h, dr) + 1:
-                            ag_send(i, h, dr, s)
-
-        for i in order:
-            unpack(i, stage_in, stage_out, flat)
-        for cp in out_copies:
-            cp.wait()
-
-        for cp in pending:
-            cp.wait_send()
-        for i in order:
-            d2d_copy(i).wait_send()
-            nrm_wait(i, s_nrm.at[i])
-            for m in range(waves[i]["cnt"]):
-                owner = (waves[i]["base"] + m) % n
-
-                @pl.when(me != owner)
-                def _():
-                    x_copy(i, m).wait_send()
-            mine, yes = owned(i)
-
-            @pl.when(yes)
+    def rs_stage(i, s):
+        for h in range(2):
+            for dr in range(2):
+                if s <= hops(h, dr):
+                    rs_send(i, h, dr, s)
+
+    def ag_stage(i, s):
+        for h in range(2):
+            for dr in range(2):
+                if s <= hops(h, dr) + 1:
+                    ag_send(i, h, dr, s)
+
+    start_loads()
+    pack(0)
+    pack(1)
+    rs_stage(0, 1)
+    native_inputs(0)
+    rs_stage(0, 2)
+    pack(2)
+    rs_stage(0, 3)
+    rs_stage(1, 1)
+    pack(3)
+    rs_stage(0, 4)
+    rs_stage(1, 2)
+    native_inputs(1)
+    rs_stage(1, 3)
+    rs_stage(2, 1)
+    rs_finish(0)
+    rs_stage(1, 4)
+    rs_stage(2, 2)
+    x_send(0)
+    rs_stage(2, 3)
+    rs_stage(3, 1)
+    rs_finish(1)
+    owner_work(0, True, 1, False)
+    x_send(1)
+    rs_stage(2, 4)
+    rs_stage(3, 2)
+    owner_work(0, False, 2, False)
+    rs_stage(3, 3)
+    rs_finish(2)
+    owner_work(0, False, NS_STEPS - 3, True)
+    rs_stage(3, 4)
+    x_send(2)
+    owner_work(1, True, NS_STEPS, True)
+    master(0)
+    ag_stage(0, 1)
+    rs_finish(3)
+    ag_stage(0, 2)
+    owner_work(2, True, NS_STEPS, True)
+    x_send(3)
+    master(1)
+    ag_stage(1, 1)
+    ag_stage(0, 3)
+    owner_work(3, True, NS_STEPS, True)
+    master(2)
+    ag_stage(2, 1)
+    ag_stage(1, 2)
+    ag_stage(0, 4)
+    master(3)
+    ag_stage(3, 1)
+    ag_stage(2, 2)
+    ag_stage(1, 3)
+    ag_stage(0, 5)
+    native_outputs(0)
+    ag_stage(3, 2)
+    ag_stage(2, 3)
+    ag_stage(1, 4)
+    native_outputs(1)
+    ag_stage(3, 3)
+    ag_stage(2, 4)
+    ag_stage(1, 5)
+    unpack(0)
+    ag_stage(3, 4)
+    ag_stage(2, 5)
+    unpack(1)
+    ag_stage(3, 5)
+    unpack(2)
+    unpack(3)
+
+    for cp in out_copies:
+        cp.wait()
+    for cp in pending:
+        cp.wait_send()
+    for i in range(n_waves):
+        for k in range(nz):
+            d2d_copy(i, k).wait_send()
+        nrm_wait(i, s_nrm.at[i])
+        for m in range(waves[i]["cnt"]):
+            owner = (waves[i]["base"] + m) % n
+
+            @pl.when(me != owner)
             def _():
-                view = otx[i].at[pl.ds(0, n - 1)]
-                pltpu.make_async_copy(view, view, s_o.at[i]).wait()
-
-    pl.run_scoped(main_phase, pltpu.VMEM((c_in, narrow, wide), BF16), pltpu.VMEM((c_out, narrow, wide), BF16),
-                  pltpu.VMEM((narrow, wide), F32))
+                x_copy(i, m).wait_send()
+        mine, yes = owned(i)
+
+        @pl.when(yes)
+        def _():
+            view = otx[i].at[pl.ds(0, n - 1)]
+            pltpu.make_async_copy(view, view, s_o.at[i]).wait()
 
 
 def hand_over(shapes):
@@ -618,7 +679,12 @@
             vm((n * attn_rows, wide), BF16),
             vm((n * attn_rows, n * attn_rows), BF16),
             vm((n * attn_rows, n * attn_rows), BF16),
-            dma(6), dma(2, 5), dma(2, 4), dma(4, 4, hops), dma(4, 4, hops),
+            vm((c_in, narrow, wide), F32),
+            vm((c_out, narrow, wide), F32),
+            vm((c_in, narrow, wide), BF16),
+            vm((c_out, narrow, wide), BF16),
+            vm((narrow, wide), F32),
+            dma(6), dma(2, 5), dma(2, 4, nz), dma(4, 4, hops), dma(4, 4, hops),
             dma(4), dma(4), dma(4, max(w_cnt)), dma(4), dma(4), dma(4),
             dma(4, 4, hops), dma(4, 4, hops), dma(4, 2, nz), dma(4, 2, nz),
             dma(15 + c_attn * tiles),

time: 178 us -> 185 us (1.039)
  Pallas kernels: 177 us -> 184 us
    pallas_call x2, Pallas kernels: 177 us -> 184 us  [local_step(): outs = list(hand_over(out_shape)(*call(*grads, *moms, *masters)))]
where the time goes in v3:
time: 185 us
  Pallas kernels  184 us (99%)
    pallas_call x2, Pallas kernels, local_step(): outs = list(hand_over(out_shape)(*call(*grads, *moms, *masters)))  184 us

profile of v3, /device:TPU:21, one launch (start us, length us, event | category | flops | bytes accessed | tf_op | source)
XLA Modules:
  0.0 185.0 jit_solution(7230982455360383569)
XLA Ops:
  0.7 177.1 %muon_step.1 = (f32[4,32,512]{2,1,0:T(8,128)}, f32[2,32,176]{2,1,0:T(8,128)}, f32[11,1,512]{2,1,0:T(1,128)}, f32[16,32,176]{2,1,0:T(8,128)}, f32[11,8,512]{2,1,0...) custom-call(f32[4,8,2,32,512]{4,3,2,1,0:T(8,128)} %bitcast.21, ...), custom_call_target="tpu_custom_call" | custom-call | tf_op jit(solution)/shard_map/muon_step/pallas_call | solution.py:703
  177.7 7.1 %hand_over.1 = (f32[4,32,512]{2,1,0:T(8,128)}, f32[2,32,176]{2,1,0:T(8,128)}, f32[11,1,512]{2,1,0:T(1,128)}, f32[16,32,176]{2,1,0:T(8,128)}, f32[11,8,512]{2,1,0...) custom-call(f32[4,32,512]{2,1,0:T(8,128)} %get-tuple-element.45.refs, ...), custom_call_target="tpu_custom_call" | custom-call | tf_op jit(solution)/shard_map/hand_over/pallas_call | solution.py:703

commit v4 on v3

--- a/solution.py
+++ b/solution.py
@@ -15,6 +15,24 @@
 COEF_A = 3.4445
 COEF_B = -4.7750
 COEF_C = 2.0315
+
+SCHEDULE = (
+    ("pack", 0), ("rs", 0, 0, 1), ("pack", 1), ("rs", 0, 1, 1), ("rs", 0, 0, 2), ("rs", 0, 1, 2), ("pack", 2),
+    ("rs", 0, 0, 3), ("nat", 1), ("rs", 0, 1, 3), ("rs", 1, 0, 1), ("rs", 0, 0, 4), ("nat", 0), ("rs", 0, 1, 4),
+    ("rs", 1, 1, 1), ("pack", 3), ("fin", 0), ("rs", 1, 0, 2), ("rs", 1, 1, 2), ("rs", 1, 0, 3), ("rs", 2, 0, 1),
+    ("rs", 1, 0, 4), ("rs", 2, 1, 1), ("rs", 1, 1, 3), ("rs", 1, 1, 4), ("x", 0), ("rs", 2, 0, 2), ("rs", 2, 1, 2),
+    ("rs", 3, 1, 1), ("fin", 1), ("own", 0, 1), ("rs", 2, 0, 3), ("own", 0, 2), ("rs", 2, 1, 3), ("rs", 3, 0, 1),
+    ("own", 0, 3), ("rs", 2, 0, 4), ("rs", 2, 1, 4), ("x", 1), ("fin", 2), ("rs", 3, 0, 2), ("rs", 3, 1, 2),
+    ("mas", 0), ("rs", 3, 0, 3), ("rs", 3, 1, 3), ("ag", 0, 1, 1), ("own", 1, 0), ("rs", 3, 0, 4), ("rs", 3, 1, 4),
+    ("x", 2), ("ag", 0, 0, 1), ("fin", 3), ("ag", 0, 0, 2), ("ag", 0, 1, 2), ("mas", 1), ("ag", 1, 0, 1),
+    ("ag", 1, 1, 1), ("own", 2, 0), ("x", 3), ("ag", 0, 0, 3), ("ag", 0, 1, 3), ("ag", 1, 0, 2), ("ag", 0, 0, 4),
+    ("ag", 1, 1, 2), ("mas", 2), ("ag", 2, 0, 1), ("ag", 2, 1, 1), ("own", 3, 0), ("ag", 1, 1, 3), ("ag", 0, 1, 4),
+    ("natout", 0), ("ag", 0, 0, 5), ("ag", 1, 0, 3), ("ag", 2, 0, 2), ("ag", 0, 1, 5), ("ag", 2, 1, 2), ("mas", 3),
+    ("ag", 3, 1, 1), ("ag", 3, 0, 1), ("ag", 2, 0, 3), ("ag", 1, 1, 4), ("ag", 2, 1, 3), ("ag", 1, 0, 4),
+    ("ag", 3, 0, 2), ("ag", 3, 1, 2), ("ag", 1, 1, 5), ("ag", 2, 0, 4), ("ag", 1, 0, 5), ("ag", 2, 1, 4),
+    ("natout", 1), ("un", 0), ("ag", 3, 1, 3), ("ag", 3, 0, 3), ("un", 1), ("ag", 2, 0, 5), ("ag", 2, 1, 5),
+    ("ag", 3, 0, 4), ("ag", 3, 1, 4), ("un", 2), ("ag", 3, 0, 5), ("ag", 3, 1, 5), ("un", 3),
+)
 
 F32 = jnp.float32
 BF16 = jnp.bfloat16
@@ -38,9 +56,9 @@
     out_rows = narrow // n
     out_pad = round_up(out_rows, 16)
     attn_blk = attn_rows * tiles
-    small_blk = round_up(tiles * out_rows, 16)
+    out_blk = tiles * out_rows
+    small_blk = round_up(out_blk, 16)
     cuts = [(q * small_blk, min(small_blk, narrow - q * small_blk)) for q in range(groups)]
-    small0 = c_attn * attn_blk
 
     it = iter(refs)
     take = lambda k: [next(it) for _ in range(k)]
@@ -51,22 +69,29 @@
     w_out = take(5)
     p_attn, p_si, p_so, p_ei, p_eo = take(5)
     (gp, rx0, rxr, ag, mp, wp, nat_m, nat_w, nrm, xtx, rxx, otx, rxo, xb, ab, bb,
-     raw_in, raw_out, stage_in, stage_out, flat) = take(21)
+     raw_in, raw_out, stage_in, stage_out) = take(20)
     (s_load, s_nat, s_d2d, s_rs, r_rs, s_nrm, r_nrm, s_x, r_x, s_o, r_o, s_ag, r_ag, s_agd, r_agd, s_out) = take(16)
 
-    in_w = c_in // 2
-    waves = []
-    base = 0
-    for kind, first, cnt in (("in", 0, in_w), ("in", in_w, c_in - in_w), ("out", c_in, c_out)):
-        waves.append(dict(kind=kind, first=first, cnt=cnt, row0=small0 + first * small_blk, blk=small_blk, base=base % n))
-        base += cnt
-    waves.insert(0, dict(kind="attn", first=0, cnt=c_attn, row0=0, blk=attn_blk, base=base % n))
+    quad = narrow
+    n_quads = c_ei // groups
+    quads_b = n_quads // 2
+    mats_b, mats_c = c_si + groups * quads_b, groups * (n_quads - quads_b)
+    rows_b, rows_c = c_si * small_blk + quads_b * quad, (n_quads - quads_b) * quad
+    rows_d = round_up(c_out * out_blk, 16)
+    waves = [dict(kind="attn", cnt=c_attn, rows=c_attn * attn_blk, base=(c_in + c_out) % n),
+             dict(kind="in", cnt=mats_b, rows=rows_b, base=0, shared=c_si, quads=quads_b, first=0),
+             dict(kind="in", cnt=mats_c, rows=rows_c, base=mats_b % n, shared=0, quads=n_quads - quads_b, first=quads_b),
+             dict(kind="out", cnt=c_out, rows=rows_d, base=c_in % n)]
     n_waves = len(waves)
+    start = 0
     for w in waves:
-        w["rows"] = w["cnt"] * w["blk"]
+        w["row0"] = start
+        start += w["rows"]
         w["half"] = w["rows"] // 2
         w["off"] = w["row0"] // 2
         w["ag_half"] = round_up(w["half"], 16)
+        w["quad0"] = w["row0"] + w.get("shared", 0) * small_blk
+    out0 = waves[3]["row0"]
 
     me = lax.axis_index("data")
     z = me // 2
@@ -98,8 +123,13 @@
             for q in range(groups):
                 if (q // dist) % 2 == 0:
                     x, y = blocks[q], blocks[q + dist]
-                    blocks[q] = jnp.where(low, x, pltpu.roll(y, width, axis=1))
-                    blocks[q + dist] = jnp.where(low, pltpu.roll(x, LANE - width, axis=1), y)
+                    if 2 * width == LANE:
+                        turned = pltpu.roll(jnp.where(low, y, x), width, axis=1)
+                        blocks[q] = jnp.where(low, x, turned)
+                        blocks[q + dist] = jnp.where(low, turned, y)
+                    else:
+                        blocks[q] = jnp.where(low, x, pltpu.roll(y, width, axis=1))
+                        blocks[q + dist] = jnp.where(low, pltpu.roll(x, LANE - width, axis=1), y)
             dist //= 2
         return blocks
 
@@ -108,15 +138,15 @@
             return x
         return jnp.concatenate([x, jnp.zeros((rows - x.shape[0], x.shape[1]), x.dtype)], axis=0)
 
-    k_cut = in_w - c_si
+    cut_in, cut_out = groups * quads_b, c_eo // groups
 
     def loads():
         return [
             pltpu.make_async_copy(g_si, raw_in.at[pl.ds(0, c_si)], s_load.at[1]),
-            pltpu.make_async_copy(g_ei.at[pl.ds(0, k_cut)], raw_in.at[pl.ds(c_si, k_cut)], s_load.at[2]),
-            pltpu.make_async_copy(g_ei.at[pl.ds(k_cut, c_ei - k_cut)], raw_in.at[pl.ds(in_w, c_ei - k_cut)], s_load.at[3]),
-            pltpu.make_async_copy(g_so, raw_out.at[pl.ds(0, c_so)], s_load.at[4]),
-            pltpu.make_async_copy(g_eo, raw_out.at[pl.ds(c_so, c_eo)], s_load.at[5]),
+            pltpu.make_async_copy(g_ei.at[pl.ds(0, cut_in)], raw_in.at[pl.ds(c_si, cut_in)], s_load.at[2]),
+            pltpu.make_async_copy(g_ei.at[pl.ds(cut_in, c_ei - cut_in)], raw_in.at[pl.ds(c_si + cut_in, c_ei - cut_in)], s_load.at[3]),
+            pltpu.make_async_copy(g_so, raw_out.at[pl.ds(c_eo, c_so)], s_load.at[4]),
+            pltpu.make_async_copy(g_eo, raw_out.at[pl.ds(0, c_eo)], s_load.at[5]),
         ]
 
     def start_loads():
@@ -128,40 +158,62 @@
         for cp in loads() + nat_copies():
             cp.start()
 
-    def pack_in(j, carry):
-        off = pl.multiple_of(small0 + small_blk * j, 8)
-        for t in range(tiles):
-            cols = slice(LANE * t, LANE * (t + 1))
-            got = lane_swap([pad_rows(raw_in[j, r:r + k, cols], small_blk) for r, k in cuts])
-            for p in range(groups):
-                d = groups * t + p
-                gp[d // 2, d % 2, pl.ds(off, small_blk), :] = got[p]
-        return carry
-
-    def pack_out(j, carry):
-        off = pl.multiple_of(small0 + small_blk * (c_in + j), 8)
+    def pack_in(i):
+        w = waves[i]
+        for j in range(w["shared"]):
+            for t in range(tiles):
+                cols = slice(LANE * t, LANE * (t + 1))
+                got = lane_swap([pad_rows(raw_in[j, r:r + k, cols], small_blk) for r, k in cuts])
+                for p in range(groups):
+                    d = groups * t + p
+                    gp[d // 2, d % 2, pl.ds(w["row0"] + small_blk * j, small_blk), :] = got[p]
+
+        def body(j, carry):
+            off = pl.multiple_of(w["quad0"] + quad * j, 8)
+            first = c_si + groups * (w["first"] + j)
+            for t in range(tiles):
+                got = lane_swap([raw_in[first + p, :, LANE * t:LANE * (t + 1)] for p in range(groups)])
+                for p in range(groups):
+                    d = groups * t + p
+                    gp[d // 2, d % 2, pl.ds(off, quad), :] = got[p]
+            return carry
+
+        lax.fori_loop(0, w["quads"], body, 0)
+
+    def out_piece(m, d):
+        return [raw_out[m, out_rows * d:out_rows * (d + 1), LANE * t:LANE * (t + 1)] for t in range(tiles)]
+
+    def pack_out():
+        def body(j, carry):
+            off = pl.multiple_of(out0 + groups * out_blk * j, 8)
+            for d in range(n):
+                rows = sum([out_piece(groups * j + p, d) for p in range(groups)], [])
+                gp[d // 2, d % 2, pl.ds(off, groups * out_blk), :] = jnp.concatenate(rows, axis=0)
+            return carry
+
+        lax.fori_loop(0, cut_out, body, 0)
+        tail = rows_d - c_eo * out_blk
         for d in range(n):
-            rows = [raw_out[j, out_rows * d:out_rows * (d + 1), LANE * t:LANE * (t + 1)] for t in range(tiles)]
-            gp[d // 2, d % 2, pl.ds(off, small_blk), :] = pad_rows(jnp.concatenate(rows, axis=0), small_blk)
-        return carry
+            rows = sum([out_piece(m, d) for m in range(c_eo, c_out)], [])
+            gp[d // 2, d % 2, pl.ds(out0 + c_eo * out_blk, tail), :] = pad_rows(jnp.concatenate(rows, axis=0), tail)
 
     def pack(i):
-        load = loads()
+        load = loads
         if i == 0:
-            view = gp.at[:, :, pl.ds(0, small0), :]
+            view = gp.at[:, :, pl.ds(0, waves[0]["rows"]), :]
             pltpu.make_async_copy(view, view, s_load.at[0]).wait()
             pl.semaphore_wait(barrier, n - 1)
         elif i == 1:
-            load[0].wait()
-            load[1].wait()
-            lax.fori_loop(0, in_w, pack_in, 0)
+            load()[0].wait()
+            load()[1].wait()
+            pack_in(1)
         elif i == 2:
-            load[2].wait()
-            lax.fori_loop(in_w, c_in, pack_in, 0)
+            load()[2].wait()
+            pack_in(2)
         else:
-            load[3].wait()
-            load[4].wait()
-            lax.fori_loop(0, c_out, pack_out, 0)
+            load()[3].wait()
+            load()[4].wait()
+            pack_out()
         for k in near_last:
             d2d_copy(i, k).start()
 
@@ -182,6 +234,17 @@
         if (i, k) not in d2d_seen:
             d2d_seen.add((i, k))
             d2d_copy(i, k).wait_recv()
+
+    def mat_rows(i):
+        w = waves[i]
+        if w["kind"] == "attn":
+            return [(m, pl.ds(attn_blk * m, attn_blk), None) for m in range(w["cnt"])]
+        if w["kind"] == "out":
+            return [(m, pl.ds(out0 + out_blk * m, out_blk), None) for m in range(w["cnt"])]
+        got = [(m, pl.ds(w["row0"] + small_blk * m, small_blk), None) for m in range(w["shared"])]
+        for j in range(w["quads"]):
+            got += [(w["shared"] + groups * j + p, pl.ds(w["quad0"] + quad * j, quad), p) for p in range(groups)]
+        return got
 
     hops = lambda h, dr: hops_far if h == dr else hops_near
     rs = {}
@@ -220,10 +283,12 @@
             mp[sl, :] = MOMENTUM * mp[sl, :] + total / n
         lane = lax.broadcasted_iota(jnp.int32, (1, LANE), 1)
         part = jnp.zeros((1, LANE), F32)
-        for m in range(w["cnt"]):
-            block = mp[pl.ds(w["row0"] + m * w["blk"], w["blk"]), :]
-            sq = jnp.sum(jnp.sum(block * block, axis=0, keepdims=True), axis=1, keepdims=True)
-            part = jnp.where(lane == m, sq, part)
+        for m, where, keep in mat_rows(i):
+            block = mp[where, :]
+            sq = jnp.sum(block * block, axis=0, keepdims=True)
+            if keep is not None:
+                sq = jnp.where(lane // in_rows == keep, sq, 0.0)
+            part = jnp.where(lane == m, jnp.sum(sq, axis=1, keepdims=True), part)
         nrm[i, me] = part
         for d in others:
             remote(nrm.at[i, me], nrm.at[i, me], s_nrm.at[i], r_nrm.at[i], {"data": d}).start()
@@ -244,15 +309,29 @@
         for d in range(n):
             tot = tot + nrm[i, d]
         lane = lax.broadcasted_iota(jnp.int32, (1, LANE), 1)
-        for m in range(w["cnt"]):
-            sq = jnp.sum(jnp.where(lane == m, tot, 0.0), axis=1, keepdims=True)
-            x = mp[pl.ds(w["row0"] + m * w["blk"], w["blk"]), :] / (jnp.sqrt(sq) + NORM_EPS)
-            if w["kind"] == "out":
-                zero = jnp.zeros((out_pad - out_rows, LANE), F32)
-                parts = []
-                for t in range(tiles):
-                    parts += [x[t * out_rows:(t + 1) * out_rows], zero]
-                x = jnp.concatenate(parts, axis=0)
+        norms = [jnp.sqrt(jnp.sum(jnp.where(lane == m, tot, 0.0), axis=1, keepdims=True)) + NORM_EPS for m in range(w["cnt"])]
+        blocks = []
+        if w["kind"] == "in":
+            for m in range(w["shared"]):
+                blocks.append(mp[pl.ds(w["row0"] + small_blk * m, small_blk), :] / norms[m])
+            for j in range(w["quads"]):
+                m = w["shared"] + groups * j
+                norm = norms[m]
+                for p in range(1, groups):
+                    norm = jnp.where(lane // in_rows == p, norms[m + p], norm)
+                x = mp[pl.ds(w["quad0"] + quad * j, quad), :] / norm
+                blocks += lane_swap([pad_rows(x[r:r + k], small_blk) for r, k in cuts])
+        else:
+            for m, where, _ in mat_rows(i):
+                x = mp[where, :] / norms[m]
+                if w["kind"] == "out":
+                    zero = jnp.zeros((out_pad - out_rows, LANE), F32)
+                    parts = []
+                    for t in range(tiles):
+                        parts += [x[t * out_rows:(t + 1) * out_rows], zero]
+                    x = jnp.concatenate(parts, axis=0)
+                blocks.append(x)
+        for m, x in enumerate(blocks):
             x = x.astype(BF16)
             xtx[i][m] = x
             owner = (w["base"] + m) % n
@@ -356,17 +435,27 @@
             pltpu.make_async_copy(rxo[i], rxo[i], r_o.at[i]).wait()
 
         step_scale = 0.2 * math.sqrt(wide)
-        for m in range(cnt):
-            sl = pl.ds(w["row0"] + m * w["blk"], w["blk"])
-            o = rxo[i][m].astype(F32)
-            if w["kind"] == "out":
-                parts = [o[out_pad * t:out_pad * t + out_rows] for t in range(tiles)]
-                parts.append(jnp.zeros((small_blk - tiles * out_rows, LANE), F32))
-                o = jnp.concatenate(parts, axis=0)
-            old = wp[sl, :]
-            new = old - LEARN_RATE * (step_scale * o + WEIGHT_DECAY * old)
-            wp[sl, :] = new
-            ag[z, c, sl, :] = new.astype(BF16)
+
+        def update(where, o):
+            old = wp[where, :]
+            wp[where, :] = old - LEARN_RATE * (step_scale * o + WEIGHT_DECAY * old)
+
+        if w["kind"] == "in":
+            for m in range(w["shared"]):
+                update(pl.ds(w["row0"] + small_blk * m, small_blk), rxo[i][m].astype(F32))
+            for j in range(w["quads"]):
+                m = w["shared"] + groups * j
+                got = lane_swap([rxo[i][m + p].astype(F32) for p in range(groups)])
+                o = jnp.concatenate([got[q][:k] for q, (r, k) in enumerate(cuts)], axis=0)
+                update(pl.ds(w["quad0"] + quad * j, quad), o)
+        else:
+            for m, where, _ in mat_rows(i):
+                o = rxo[i][m].astype(F32)
+                if w["kind"] == "out":
+                    o = jnp.concatenate([o[out_pad * t:out_pad * t + out_rows] for t in range(tiles)], axis=0)
+                update(where, o)
+        sl = pl.ds(w["row0"], w["rows"])
+        ag[z, c, sl, :] = wp[sl, :].astype(BF16)
 
     agc = {}
     agd = {}
@@ -408,28 +497,31 @@
         cp.start()
         out_copies.append(cp)
 
+    def quad_row(j):
+        return waves[1]["quad0"] + quad * j if j < quads_b else waves[2]["quad0"] + quad * (j - quads_b)
+
+    def out_rows_of():
+        return [(4, m, out0 + out_blk * m) for m in range(c_eo)] + [(2, m, out0 + out_blk * (c_eo + m)) for m in range(c_so)]
+
     def native_outputs(which):
         for src, nat, outs in (((mp, nat_m, m_out), (wp, nat_w, w_out))[which],):
             for m in range(c_attn):
                 for t in range(tiles):
                     nat[0][m, :, LANE * t:LANE * (t + 1)] = src[pl.ds(m * attn_blk + t * attn_rows, attn_rows), :]
-            j = 0
-            for k, cnt in ((1, c_si), (3, c_ei)):
-                for m in range(0, cnt, groups):
-                    some = min(groups, cnt - m)
-                    off = small0 + small_blk * (j + m)
-                    got = [src[off + small_blk * p:off + small_blk * (p + 1), :] for p in range(some)]
-                    got += [jnp.zeros((small_blk, LANE), F32)] * (groups - some)
-                    block = pad_rows(jnp.concatenate(lane_swap(got), axis=0), 2 * LANE).T
-                    for p in range(some):
-                        nat[k][m + p] = block[in_rows * p:in_rows * (p + 1), :narrow]
-                j += cnt
-            for k, cnt in ((2, c_so), (4, c_eo)):
-                for m in range(cnt):
-                    off = small0 + small_blk * j
-                    for t in range(tiles):
-                        nat[k][:, m, LANE * t:LANE * (t + 1)] = src[off + t * out_rows:off + (t + 1) * out_rows, :]
-                    j += 1
+            some = c_si
+            off = waves[1]["row0"]
+            got = [src[off + small_blk * p:off + small_blk * (p + 1), :] for p in range(some)]
+            got += [jnp.zeros((small_blk, LANE), F32)] * (groups - some)
+            block = pad_rows(jnp.concatenate(lane_swap(got), axis=0), 2 * LANE).T
+            for p in range(some):
+                nat[1][p] = block[in_rows * p:in_rows * (p + 1), :narrow]
+            for j in range(n_quads):
+                block = pad_rows(src[pl.ds(quad_row(j), quad), :], 2 * LANE).T
+                for p in range(groups):
+                    nat[3][groups * j + p] = block[in_rows * p:in_rows * (p + 1), :narrow]
+            for k, m, off in out_rows_of():
+                for t in range(tiles):
+                    nat[k][:, m, LANE * t:LANE * (t + 1)] = src[off + t * out_rows:off + (t + 1) * out_rows, :]
             for k in range(5):
                 out_copy(nat[k], outs[k], which * 5 + k)
 
@@ -440,21 +532,21 @@
             for m in range(c_attn):
                 for t in range(tiles):
                     dst[pl.ds(m * attn_blk + t * attn_rows, attn_rows), :] = nat[0][m, :, LANE * t:LANE * (t + 1)]
-            j = 0
-            for k, cnt in ((1, c_si), (3, c_ei)):
-                for m in range(0, cnt, groups):
-                    some = min(groups, cnt - m)
-                    block = pad_rows(jnp.concatenate([nat[k][m + p] for p in range(some)], axis=0), LANE)
-                    block = jnp.concatenate([block, jnp.zeros((LANE, 2 * LANE - narrow), F32)], axis=1).T
-                    got = lane_swap([block[small_blk * q:small_blk * (q + 1)] for q in range(groups)])
-                    for p in range(some):
-                        dst[pl.ds(small0 + small_blk * (j + m + p), small_blk), :] = got[p]
-                j += cnt
-            for k, cnt in ((2, c_so), (4, c_eo)):
-                for m in range(cnt):
-                    rows = [nat[k][:, m, LANE * t:LANE * (t + 1)] for t in range(tiles)]
-                    dst[pl.ds(small0 + small_blk * j, small_blk), :] = pad_rows(jnp.concatenate(rows, axis=0), small_blk)
-                    j += 1
+            wider = lambda x: jnp.concatenate([x, jnp.zeros((LANE, 2 * LANE - narrow), F32)], axis=1)
+            block = pad_rows(jnp.concatenate([nat[1][p] for p in range(c_si)], axis=0), LANE)
+            block = wider(block).T
+            got = lane_swap([block[small_blk * q:small_blk * (q + 1)] for q in range(groups)])
+            for p in range(c_si):
+                dst[pl.ds(waves[1]["row0"] + small_blk * p, small_blk), :] = got[p]
+            for j in range(n_quads):
+                block = jnp.concatenate([nat[3][groups * j + p] for p in range(groups)], axis=0)
+                dst[pl.ds(quad_row(j), quad), :] = wider(block).T[:quad]
+            for k, m, off in out_rows_of():
+                rows = [nat[k][:, m, LANE * t:LANE * (t + 1)] for t in range(tiles)]
+                dst[pl.ds(off, out_blk), :] = jnp.concatenate(rows, axis=0)
+            spare = rows_d - c_out * out_blk
+            if spare:
+                dst[pl.ds(out0 + c_out * out_blk, spare), :] = jnp.zeros((spare, LANE), F32)
 
     def unpack(i):
         w = waves[i]
@@ -469,114 +561,71 @@
                         p_attn.at[m, :, :, :, pl.ds(LANE * t, LANE)], s_out.at[10 + m * tiles + t]))
                     out_copies[-1].start()
         elif w["kind"] == "in":
-            def body(j, carry):
-                off = pl.multiple_of(small0 + small_blk * j, 16)
+            for j in range(w["shared"]):
+                sl = pl.ds(w["row0"] + small_blk * j, small_blk)
                 for t in range(tiles):
                     devs = [groups * t + p for p in range(groups)]
-                    got = lane_swap([ag[d // 2, d % 2, pl.ds(off, small_blk), :].astype(F32) for d in devs])
+                    got = lane_swap([ag[d // 2, d % 2, sl, :].astype(F32) for d in devs])
                     for q, (r, k) in enumerate(cuts):
                         stage_in[j, r:r + k, LANE * t:LANE * (t + 1)] = got[q][:k].astype(BF16)
+
+            def body(j, carry):
+                off = pl.multiple_of(w["quad0"] + quad * j, 16)
+                first = c_si + groups * (w["first"] + j)
+                for t in range(tiles):
+                    devs = [groups * t + p for p in range(groups)]
+                    got = lane_swap([ag[d // 2, d % 2, pl.ds(off, quad), :].astype(F32) for d in devs])
+                    for p in range(groups):
+                        stage_in[first + p, :, LANE * t:LANE * (t + 1)] = got[p].astype(BF16)
                 return carry
-            lax.fori_loop(w["first"], w["first"] + w["cnt"], body, 0)
+
+            lax.fori_loop(0, w["quads"], body, 0)
             k = 10 + c_attn * tiles
-            if w["first"] == 0:
+            if w["shared"]:
                 out_copy(stage_in.at[pl.ds(0, c_si)], p_si, k)
-                out_copy(stage_in.at[pl.ds(c_si, in_w - c_si)], p_ei.at[pl.ds(0, in_w - c_si)], k + 1)
-            else:
-                out_copy(stage_in.at[pl.ds(in_w, c_in - in_w)], p_ei.at[pl.ds(in_w - c_si, c_in - in_w)], k + 2)
+            first, cnt = groups * w["first"], groups * w["quads"]
+            out_copy(stage_in.at[pl.ds(c_si + first, cnt)], p_ei.at[pl.ds(first, cnt)], k + 1 + (w["first"] > 0))
         else:
+            def put(blk, m, first, d):
+                for t in range(tiles):
+                    r = out_blk * m + t * out_rows
+                    raw_out[first + m, out_rows * d:out_rows * (d + 1), LANE * t:LANE * (t + 1)] = blk[r:r + out_rows]
+
             def body(j, carry):
-                off = pl.multiple_of(small0 + small_blk * (c_in + j), 16)
+                off = pl.multiple_of(out0 + groups * out_blk * j, 16)
                 for d in range(n):
-                    blk = ag[d // 2, d % 2, pl.ds(off, small_blk), :].astype(F32)
-                    for t in range(tiles):
-                        flat[out_rows * d:out_rows * (d + 1), LANE * t:LANE * (t + 1)] = blk[t * out_rows:(t + 1) * out_rows]
-                stage_out[j] = flat[...].astype(BF16)
+                    blk = ag[d // 2, d % 2, pl.ds(off, groups * out_blk), :].astype(F32)
+                    for p in range(groups):
+                        put(blk, p, groups * j, d)
+                for p in range(groups):
+                    stage_out[groups * j + p] = raw_out[groups * j + p].astype(BF16)
                 return carry
-            lax.fori_loop(0, c_out, body, 0)
+
+            lax.fori_loop(0, cut_out, body, 0)
+            for d in range(n):
+                blk = ag[d // 2, d % 2, pl.ds(out0 + c_eo * out_blk, rows_d - c_eo * out_blk), :].astype(F32)
+                for m in range(c_so):
+                    put(blk, m, c_eo, d)
+            for m in range(c_eo, c_out):
+                stage_out[m] = raw_out[m].astype(BF16)
             k = 13 + c_attn * tiles
-            out_copy(stage_out.at[pl.ds(0, c_so)], p_so, k)
-            out_copy(stage_out.at[pl.ds(c_so, c_eo)], p_eo, k + 1)
-
-    def rs_stage(i, s):
-        for h in range(2):
-            for dr in range(2):
-                if s <= hops(h, dr):
-                    rs_send(i, h, dr, s)
-
-    def ag_stage(i, s):
-        for h in range(2):
-            for dr in range(2):
-                if s <= hops(h, dr) + 1:
-                    ag_send(i, h, dr, s)
-
+            out_copy(stage_out.at[pl.ds(c_eo, c_so)], p_so, k)
+            out_copy(stage_out.at[pl.ds(0, c_eo)], p_eo, k + 1)
+
+    def both(func, length, i, h, s):
+        for dr in range(2):
+            if s <= hops(h, dr) + length:
+                func(i, h, dr, s)
+
+    def own(i, part):
+        begin, steps, end = ((True, NS_STEPS, True), (True, 1, False), (False, 2, False), (False, NS_STEPS - 3, True))[part]
+        owner_work(i, begin, steps, end)
+
+    acts = dict(pack=pack, nat=native_inputs, rs=functools.partial(both, rs_send, 0), fin=rs_finish, x=x_send, own=own,
+                mas=master, ag=functools.partial(both, ag_send, 1), natout=native_outputs, un=unpack)
     start_loads()
-    pack(0)
-    pack(1)
-    rs_stage(0, 1)
-    native_inputs(0)
-    rs_stage(0, 2)
-    pack(2)
-    rs_stage(0, 3)
-    rs_stage(1, 1)
-    pack(3)
-    rs_stage(0, 4)
-    rs_stage(1, 2)
-    native_inputs(1)
-    rs_stage(1, 3)
-    rs_stage(2, 1)
-    rs_finish(0)
-    rs_stage(1, 4)
-    rs_stage(2, 2)
-    x_send(0)
-    rs_stage(2, 3)
-    rs_stage(3, 1)
-    rs_finish(1)
-    owner_work(0, True, 1, False)
-    x_send(1)
-    rs_stage(2, 4)
-    rs_stage(3, 2)
-    owner_work(0, False, 2, False)
-    rs_stage(3, 3)
-    rs_finish(2)
-    owner_work(0, False, NS_STEPS - 3, True)
-    rs_stage(3, 4)
-    x_send(2)
-    owner_work(1, True, NS_STEPS, True)
-    master(0)
-    ag_stage(0, 1)
-    rs_finish(3)
-    ag_stage(0, 2)
-    owner_work(2, True, NS_STEPS, True)
-    x_send(3)
-    master(1)
-    ag_stage(1, 1)
-    ag_stage(0, 3)
-    owner_work(3, True, NS_STEPS, True)
-    master(2)
-    ag_stage(2, 1)
-    ag_stage(1, 2)
-    ag_stage(0, 4)
-    master(3)
-    ag_stage(3, 1)
-    ag_stage(2, 2)
-    ag_stage(1, 3)
-    ag_stage(0, 5)
-    native_outputs(0)
-    ag_stage(3, 2)
-    ag_stage(2, 3)
-    ag_stage(1, 4)
-    native_outputs(1)
-    ag_stage(3, 3)
-    ag_stage(2, 4)
-    ag_stage(1, 5)
-    unpack(0)
-    ag_stage(3, 4)
-    ag_stage(2, 5)
-    unpack(1)
-    ag_stage(3, 5)
-    unpack(2)
-    unpack(3)
+    for name, *where in SCHEDULE:
+        acts[name](*where)
 
     for cp in out_copies:
         cp.wait()
@@ -642,10 +691,13 @@
         c_attn, c_si, c_so, c_ei, c_eo = counts
         c_in, c_out = c_si + c_ei, c_so + c_eo
         tiles = wide // LANE
-        small_blk = round_up(tiles * (narrow // n), 16)
+        groups = LANE // (wide // n)
+        out_blk = tiles * (narrow // n)
+        small_blk = round_up(out_blk, 16)
         out_pad = round_up(narrow // n, 16)
         attn_blk = attn_rows * tiles
-        rows = c_attn * attn_blk + (c_in + c_out) * small_blk
+        rows = c_attn * attn_blk + c_si * small_blk + c_ei // groups * narrow + round_up(c_out * out_blk, 16)
+        mats_b = c_si + groups * (c_ei // groups // 2)
         turn = lambda x: jnp.swapaxes(x, -1, -2)
         grads = [g[0] for g in grads]
         grads[1], grads[3] = turn(grads[1]), turn(grads[3])
@@ -658,7 +710,7 @@
         out_shape = [sds(m.shape, F32) for m in moms] * 2
         out_shape += [sds((c_attn, nz, 2, attn_rows, wide), BF16)]
         out_shape += [sds((k, narrow, wide), BF16) for k in counts[1:]]
-        w_cnt = (c_attn, c_in // 2, c_in - c_in // 2, c_out)
+        w_cnt = (c_attn, mats_b, c_in - mats_b, c_out)
         w_blk = (attn_blk, small_blk, small_blk, out_pad * tiles)
         dma = lambda *shape: pltpu.SemaphoreType.DMA(shape)
         vm = pltpu.VMEM
@@ -683,7 +735,6 @@
             vm((c_out, narrow, wide), F32),
             vm((c_in, narrow, wide), BF16),
             vm((c_out, narrow, wide), BF16),
-            vm((narrow, wide), F32),
             dma(6), dma(2, 5), dma(2, 4, nz), dma(4, 4, hops), dma(4, 4, hops),
             dma(4), dma(4), dma(4, max(w_cnt)), dma(4), dma(4), dma(4),
             dma(4, 4, hops), dma(4, 4, hops), dma(4, 2, nz), dma(4, 2, nz),

time: 185 us -> 175 us (0.946)
  Pallas kernels: 184 us -> 174 us
    pallas_call x2, Pallas kernels: 184 us -> 174 us  [local_step(): outs = list(hand_over(out_shape)(*call(*grads, *moms, *masters)))]
where the time goes in v4:
time: 175 us
  Pallas kernels  174 us (99%)
    pallas_call x2, Pallas kernels, local_step(): outs = list(hand_over(out_shape)(*call(*grads, *moms, *masters)))  174 us

profile of v4, /device:TPU:21, one launch (start us, length us, event | category | flops | bytes accessed | tf_op | source)
XLA Modules:
  0.0 174.9 jit_solution(15986739167003073312)
XLA Ops:
  0.7 167.0 %muon_step.1 = (f32[4,32,512]{2,1,0:T(8,128)}, f32[2,32,176]{2,1,0:T(8,128)}, f32[11,1,512]{2,1,0:T(1,128)}, f32[16,32,176]{2,1,0:T(8,128)}, f32[11,8,512]{2,1,0...) custom-call(f32[4,8,2,32,512]{4,3,2,1,0:T(8,128)} %bitcast.21, ...), custom_call_target="tpu_custom_call" | custom-call | tf_op jit(solution)/shard_map/muon_step/pallas_call | solution.py:754
  167.7 7.1 %hand_over.1 = (f32[4,32,512]{2,1,0:T(8,128)}, f32[2,32,176]{2,1,0:T(8,128)}, f32[11,1,512]{2,1,0:T(1,128)}, f32[16,32,176]{2,1,0:T(8,128)}, f32[11,8,512]{2,1,0...) custom-call(f32[4,32,512]{2,1,0:T(8,128)} %get-tuple-element.45.refs, ...), custom_call_target="tpu_custom_call" | custom-call | tf_op jit(solution)/shard_map/hand_over/pallas_call | solution.py:754

commit v5 on v4

--- a/solution.py
+++ b/solution.py
@@ -17,22 +17,25 @@
 COEF_C = 2.0315
 
 SCHEDULE = (
-    ("pack", 0), ("rs", 0, 0, 1), ("pack", 1), ("rs", 0, 1, 1), ("rs", 0, 0, 2), ("rs", 0, 1, 2), ("pack", 2),
-    ("rs", 0, 0, 3), ("nat", 1), ("rs", 0, 1, 3), ("rs", 1, 0, 1), ("rs", 0, 0, 4), ("nat", 0), ("rs", 0, 1, 4),
-    ("rs", 1, 1, 1), ("pack", 3), ("fin", 0), ("rs", 1, 0, 2), ("rs", 1, 1, 2), ("rs", 1, 0, 3), ("rs", 2, 0, 1),
-    ("rs", 1, 0, 4), ("rs", 2, 1, 1), ("rs", 1, 1, 3), ("rs", 1, 1, 4), ("x", 0), ("rs", 2, 0, 2), ("rs", 2, 1, 2),
-    ("rs", 3, 1, 1), ("fin", 1), ("own", 0, 1), ("rs", 2, 0, 3), ("own", 0, 2), ("rs", 2, 1, 3), ("rs", 3, 0, 1),
-    ("own", 0, 3), ("rs", 2, 0, 4), ("rs", 2, 1, 4), ("x", 1), ("fin", 2), ("rs", 3, 0, 2), ("rs", 3, 1, 2),
-    ("mas", 0), ("rs", 3, 0, 3), ("rs", 3, 1, 3), ("ag", 0, 1, 1), ("own", 1, 0), ("rs", 3, 0, 4), ("rs", 3, 1, 4),
-    ("x", 2), ("ag", 0, 0, 1), ("fin", 3), ("ag", 0, 0, 2), ("ag", 0, 1, 2), ("mas", 1), ("ag", 1, 0, 1),
-    ("ag", 1, 1, 1), ("own", 2, 0), ("x", 3), ("ag", 0, 0, 3), ("ag", 0, 1, 3), ("ag", 1, 0, 2), ("ag", 0, 0, 4),
-    ("ag", 1, 1, 2), ("mas", 2), ("ag", 2, 0, 1), ("ag", 2, 1, 1), ("own", 3, 0), ("ag", 1, 1, 3), ("ag", 0, 1, 4),
-    ("natout", 0), ("ag", 0, 0, 5), ("ag", 1, 0, 3), ("ag", 2, 0, 2), ("ag", 0, 1, 5), ("ag", 2, 1, 2), ("mas", 3),
-    ("ag", 3, 1, 1), ("ag", 3, 0, 1), ("ag", 2, 0, 3), ("ag", 1, 1, 4), ("ag", 2, 1, 3), ("ag", 1, 0, 4),
-    ("ag", 3, 0, 2), ("ag", 3, 1, 2), ("ag", 1, 1, 5), ("ag", 2, 0, 4), ("ag", 1, 0, 5), ("ag", 2, 1, 4),
-    ("natout", 1), ("un", 0), ("ag", 3, 1, 3), ("ag", 3, 0, 3), ("un", 1), ("ag", 2, 0, 5), ("ag", 2, 1, 5),
-    ("ag", 3, 0, 4), ("ag", 3, 1, 4), ("un", 2), ("ag", 3, 0, 5), ("ag", 3, 1, 5), ("un", 3),
+    ("pack", 0), ("rs", 0, 0, 1), ("rs", 0, 1, 1), ("pack", 1), ("rs", 0, 0, 2), ("pack", 2), ("rs", 0, 1, 2),
+    ("rs", 1, 1, 1), ("nat", 1), ("rs", 1, 0, 1), ("rs", 1, 1, 2), ("rs", 0, 1, 3), ("rs", 1, 0, 2),
+    ("rs", 0, 0, 3), ("pack", 3), ("nat", 0), ("rs", 1, 1, 3), ("rs", 0, 0, 4), ("rs", 0, 1, 4), ("rs", 3, 0, 1),
+    ("rs", 3, 1, 1), ("fin", 0), ("rs", 1, 0, 3), ("rs", 2, 1, 1), ("rs", 3, 1, 2), ("rs", 1, 1, 4),
+    ("rs", 1, 0, 4), ("rs", 3, 0, 2), ("rs", 2, 0, 1), ("rs", 3, 1, 3), ("fin", 1), ("x", 0), ("rs", 2, 1, 2),
+    ("rs", 3, 0, 3), ("rs", 2, 0, 2), ("x", 1), ("rs", 3, 1, 4), ("own", 0, 1), ("rs", 2, 1, 3), ("own", 0, 2),
+    ("rs", 3, 0, 4), ("own", 0, 3), ("own", 1, 0), ("fin", 3), ("rs", 2, 0, 3), ("rs", 2, 0, 4), ("mas", 0),
+    ("ag", 0, 1, 1), ("rs", 2, 1, 4), ("ag", 0, 0, 1), ("mas", 1), ("fin", 2), ("ag", 1, 1, 1), ("ag", 1, 0, 1),
+    ("ag", 1, 1, 2), ("x", 3), ("x", 2), ("ag", 1, 1, 3), ("ag", 0, 1, 2), ("natout", 0), ("ag", 1, 0, 2),
+    ("ag", 1, 1, 4), ("own", 2, 0), ("own", 3, 0), ("ag", 0, 0, 2), ("ag", 1, 1, 5), ("ag", 1, 0, 3), ("mas", 2),
+    ("ag", 0, 1, 3), ("ag", 2, 1, 1), ("ag", 2, 0, 1), ("mas", 3), ("ag", 1, 0, 4), ("ag", 2, 1, 2),
+    ("ag", 3, 1, 1), ("ag", 3, 0, 1), ("ag", 2, 0, 2), ("ag", 3, 1, 2), ("ag", 3, 0, 2), ("ag", 1, 0, 5),
+    ("ag", 2, 0, 3), ("ag", 2, 1, 3), ("ag", 3, 0, 3), ("ag", 3, 1, 3), ("ag", 2, 0, 4), ("ag", 2, 1, 4),
+    ("ag", 0, 0, 3), ("un", 1), ("ag", 2, 0, 5), ("ag", 0, 1, 4), ("ag", 2, 1, 5), ("ag", 3, 1, 4),
+    ("ag", 3, 0, 4), ("natout", 1), ("ag", 0, 0, 4), ("un", 2), ("ag", 3, 0, 5), ("ag", 3, 1, 5), ("ag", 0, 1, 5),
+    ("ag", 0, 0, 5), ("un", 3), ("un", 0),
 )
+
+FIRST_PART = 0.68
 
 F32 = jnp.float32
 BF16 = jnp.bfloat16
@@ -87,9 +90,8 @@
     for w in waves:
         w["row0"] = start
         start += w["rows"]
-        w["half"] = w["rows"] // 2
-        w["off"] = w["row0"] // 2
-        w["ag_half"] = round_up(w["half"], 16)
+        split = int(w["rows"] * FIRST_PART / 16 + 0.5) * 16
+        w["halves"] = (pl.ds(w["row0"], split), pl.ds(w["row0"] + split, w["rows"] - split))
         w["quad0"] = w["row0"] + w.get("shared", 0) * small_blk
     out0 = waves[3]["row0"]
 
@@ -255,15 +257,14 @@
         step = length - s + 1
         dest = zmod(z + step) if dr == 0 else zmod(z - step)
         d2d_wait(i, step if dr == 0 else nz - step)
-        sl = pl.ds(w["row0"] + h * w["half"], w["half"])
-        osl = pl.ds(w["off"], w["half"])
+        sl = w["halves"][h]
         val = gp[dest, c, sl, :] + rx0[dest, sl, :]
         if s > 1:
             rs[i, h, dr, s - 1].wait_recv()
-            val = val + rxr[dr, h, s - 2, osl, :]
+            val = val + rxr[dr, s - 2, sl, :]
         gp[dest, c, sl, :] = val
         where = dev(zmod(z + 1), c) if dr == 0 else dev(zmod(z - 1), c)
-        cp = remote(gp.at[dest, c, sl, :], rxr.at[dr, h, s - 1, osl, :],
+        cp = remote(gp.at[dest, c, sl, :], rxr.at[dr, s - 1, sl, :],
                     s_rs.at[i, h * 2 + dr, s - 1], r_rs.at[i, h * 2 + dr, s - 1], where)
         cp.start()
         rs[i, h, dr, s] = cp
@@ -273,13 +274,12 @@
         w = waves[i]
         d2d_wait(i, 0)
         for h in range(2):
-            sl = pl.ds(w["row0"] + h * w["half"], w["half"])
-            osl = pl.ds(w["off"], w["half"])
+            sl = w["halves"][h]
             total = gp[z, c, sl, :] + rx0[z, sl, :]
             for dr in range(2):
                 last = hops(h, dr)
                 rs[i, h, dr, last].wait_recv()
-                total = total + rxr[dr, h, last - 1, osl, :]
+                total = total + rxr[dr, last - 1, sl, :]
             mp[sl, :] = MOMENTUM * mp[sl, :] + total / n
         lane = lax.broadcasted_iota(jnp.int32, (1, LANE), 1)
         part = jnp.zeros((1, LANE), F32)
@@ -461,10 +461,7 @@
     agd = {}
 
     def ag_rows(i, h):
-        w = waves[i]
-        if h == 0:
-            return pl.ds(w["row0"], w["ag_half"])
-        return pl.ds(w["row0"] + w["ag_half"], w["rows"] - w["ag_half"])
+        return waves[i]["halves"][h]
 
     def ag_to_partner(i, h, src, key):
         part = ag.at[src, c, ag_rows(i, h), :]
@@ -717,7 +714,7 @@
         scratch = [
             vm((nz, 2, rows, LANE), F32),
             vm((nz, rows, LANE), F32),
-            vm((2, 2, hops, rows // 2, LANE), F32),
+            vm((2, hops, rows, LANE), F32),
             vm((nz, 2, rows, LANE), BF16),
             vm((rows, LANE), F32),
             vm((rows, LANE), F32),

time: 175 us -> 173 us (0.989)
  Pallas kernels: 174 us -> 172 us
    pallas_call x2, Pallas kernels: 174 us -> 172 us  [local_step(): outs = list(hand_over(out_shape)(*call(*grads, *moms, *masters)))]
where the time goes in v5:
time: 173 us
  Pallas kernels  172 us (99%)
    pallas_call x2, Pallas kernels, local_step(): outs = list(hand_over(out_shape)(*call(*grads, *moms, *masters)))  172 us

profile of v5, /device:TPU:21, one launch (start us, length us, event | category | flops | bytes accessed | tf_op | source)
XLA Modules:
  0.0 173.1 jit_solution(18018229261879103000)
XLA Ops:
  0.7 165.2 %muon_step.1 = (f32[4,32,512]{2,1,0:T(8,128)}, f32[2,32,176]{2,1,0:T(8,128)}, f32[11,1,512]{2,1,0:T(1,128)}, f32[16,32,176]{2,1,0:T(8,128)}, f32[11,8,512]{2,1,0...) custom-call(f32[4,8,2,32,512]{4,3,2,1,0:T(8,128)} %bitcast.21, ...), custom_call_target="tpu_custom_call" | custom-call | tf_op jit(solution)/shard_map/muon_step/pallas_call | solution.py:751
  165.9 7.1 %hand_over.1 = (f32[4,32,512]{2,1,0:T(8,128)}, f32[2,32,176]{2,1,0:T(8,128)}, f32[11,1,512]{2,1,0:T(1,128)}, f32[16,32,176]{2,1,0:T(8,128)}, f32[11,8,512]{2,1,0...) custom-call(f32[4,32,512]{2,1,0:T(8,128)} %get-tuple-element.45.refs, ...), custom_call_target="tpu_custom_call" | custom-call | tf_op jit(solution)/shard_map/hand_over/pallas_call | solution.py:751

commit v6 on v5

--- a/solution.py
+++ b/solution.py
@@ -17,25 +17,25 @@
 COEF_C = 2.0315
 
 SCHEDULE = (
-    ("pack", 0), ("rs", 0, 0, 1), ("rs", 0, 1, 1), ("pack", 1), ("rs", 0, 0, 2), ("pack", 2), ("rs", 0, 1, 2),
-    ("rs", 1, 1, 1), ("nat", 1), ("rs", 1, 0, 1), ("rs", 1, 1, 2), ("rs", 0, 1, 3), ("rs", 1, 0, 2),
-    ("rs", 0, 0, 3), ("pack", 3), ("nat", 0), ("rs", 1, 1, 3), ("rs", 0, 0, 4), ("rs", 0, 1, 4), ("rs", 3, 0, 1),
-    ("rs", 3, 1, 1), ("fin", 0), ("rs", 1, 0, 3), ("rs", 2, 1, 1), ("rs", 3, 1, 2), ("rs", 1, 1, 4),
-    ("rs", 1, 0, 4), ("rs", 3, 0, 2), ("rs", 2, 0, 1), ("rs", 3, 1, 3), ("fin", 1), ("x", 0), ("rs", 2, 1, 2),
-    ("rs", 3, 0, 3), ("rs", 2, 0, 2), ("x", 1), ("rs", 3, 1, 4), ("own", 0, 1), ("rs", 2, 1, 3), ("own", 0, 2),
-    ("rs", 3, 0, 4), ("own", 0, 3), ("own", 1, 0), ("fin", 3), ("rs", 2, 0, 3), ("rs", 2, 0, 4), ("mas", 0),
-    ("ag", 0, 1, 1), ("rs", 2, 1, 4), ("ag", 0, 0, 1), ("mas", 1), ("fin", 2), ("ag", 1, 1, 1), ("ag", 1, 0, 1),
-    ("ag", 1, 1, 2), ("x", 3), ("x", 2), ("ag", 1, 1, 3), ("ag", 0, 1, 2), ("natout", 0), ("ag", 1, 0, 2),
-    ("ag", 1, 1, 4), ("own", 2, 0), ("own", 3, 0), ("ag", 0, 0, 2), ("ag", 1, 1, 5), ("ag", 1, 0, 3), ("mas", 2),
-    ("ag", 0, 1, 3), ("ag", 2, 1, 1), ("ag", 2, 0, 1), ("mas", 3), ("ag", 1, 0, 4), ("ag", 2, 1, 2),
-    ("ag", 3, 1, 1), ("ag", 3, 0, 1), ("ag", 2, 0, 2), ("ag", 3, 1, 2), ("ag", 3, 0, 2), ("ag", 1, 0, 5),
-    ("ag", 2, 0, 3), ("ag", 2, 1, 3), ("ag", 3, 0, 3), ("ag", 3, 1, 3), ("ag", 2, 0, 4), ("ag", 2, 1, 4),
-    ("ag", 0, 0, 3), ("un", 1), ("ag", 2, 0, 5), ("ag", 0, 1, 4), ("ag", 2, 1, 5), ("ag", 3, 1, 4),
-    ("ag", 3, 0, 4), ("natout", 1), ("ag", 0, 0, 4), ("un", 2), ("ag", 3, 0, 5), ("ag", 3, 1, 5), ("ag", 0, 1, 5),
-    ("ag", 0, 0, 5), ("un", 3), ("un", 0),
+    ("pack", 0), ("rs", 0, 0, 1), ("rs", 0, 1, 1), ("pack", 1), ("rs", 1, 1, 1), ("rs", 1, 0, 1), ("rs", 0, 0, 2),
+    ("rs", 1, 1, 2), ("rs", 0, 1, 2), ("pack", 2), ("rs", 1, 0, 2), ("rs", 0, 0, 3), ("rs", 1, 0, 3),
+    ("rs", 1, 1, 3), ("nat", 0), ("rs", 0, 0, 4), ("rs", 0, 1, 3), ("pack", 3), ("rs", 1, 1, 4), ("rs", 1, 0, 4),
+    ("rs", 3, 1, 1), ("rs", 3, 0, 1), ("rs", 0, 1, 4), ("fin", 1), ("rs", 2, 0, 1), ("rs", 3, 1, 2), ("fin", 0),
+    ("rs", 2, 1, 1), ("rs", 2, 0, 2), ("rs", 3, 0, 2), ("x", 0), ("x", 1), ("rs", 3, 0, 3), ("rs", 2, 0, 3),
+    ("nat", 1), ("rs", 3, 1, 3), ("rs", 2, 1, 2), ("rs", 3, 0, 4), ("own", 0, 1), ("own", 0, 2), ("rs", 2, 0, 4),
+    ("own", 0, 3), ("own", 1, 0), ("rs", 2, 1, 3), ("rs", 3, 1, 4), ("rs", 2, 1, 4), ("mas", 1), ("ag", 1, 0, 1),
+    ("fin", 3), ("fin", 2), ("mas", 0), ("ag", 1, 1, 1), ("ag", 0, 1, 1), ("ag", 1, 0, 2), ("ag", 1, 1, 2),
+    ("x", 2), ("x", 3), ("ag", 0, 1, 2), ("ag", 1, 1, 3), ("ag", 0, 0, 1), ("own", 2, 0), ("ag", 1, 0, 3),
+    ("own", 3, 0), ("ag", 0, 0, 2), ("natout", 0), ("ag", 1, 1, 4), ("ag", 0, 1, 3), ("ag", 1, 0, 4), ("mas", 2),
+    ("ag", 2, 0, 1), ("ag", 2, 1, 1), ("mas", 3), ("ag", 3, 0, 1), ("ag", 1, 1, 5), ("ag", 3, 1, 1),
+    ("ag", 2, 0, 2), ("ag", 2, 1, 2), ("ag", 3, 0, 2), ("natout", 1), ("ag", 3, 1, 2), ("ag", 0, 1, 4),
+    ("ag", 1, 0, 5), ("ag", 2, 1, 3), ("ag", 0, 0, 3), ("ag", 2, 0, 3), ("un", 1), ("ag", 3, 1, 3),
+    ("ag", 0, 1, 5), ("ag", 3, 0, 3), ("ag", 2, 1, 4), ("ag", 2, 0, 4), ("ag", 0, 0, 4), ("ag", 3, 1, 4),
+    ("ag", 3, 0, 4), ("ag", 2, 0, 5), ("ag", 2, 1, 5), ("ag", 0, 0, 5), ("ag", 3, 1, 5), ("ag", 3, 0, 5),
+    ("un", 2), ("un", 3), ("un", 0),
 )
 
-FIRST_PART = 0.68
+FIRST_PART = 0.5
 
 F32 = jnp.float32
 BF16 = jnp.bfloat16
@@ -324,13 +324,7 @@
         else:
             for m, where, _ in mat_rows(i):
                 x = mp[where, :] / norms[m]
-                if w["kind"] == "out":
-                    zero = jnp.zeros((out_pad - out_rows, LANE), F32)
-                    parts = []
-                    for t in range(tiles):
-                        parts += [x[t * out_rows:(t + 1) * out_rows], zero]
-                    x = jnp.concatenate(parts, axis=0)
-                blocks.append(x)
+                blocks.append(pad_rows(x, small_blk) if w["kind"] == "out" else x)
         for m, x in enumerate(blocks):
             x = x.astype(BF16)
             xtx[i][m] = x
@@ -356,8 +350,11 @@
             for t in range(tiles):
                 xb[:, LANE * t:LANE * (t + 1)] = rx[:, attn_rows * t:attn_rows * (t + 1), :].reshape(n * attn_rows, LANE)
         elif kind == "out":
-            for t in range(tiles):
-                xb[:n * out_pad, LANE * t:LANE * (t + 1)] = rx[:, out_pad * t:out_pad * (t + 1), :].reshape(n * out_pad, LANE)
+            for d in range(n):
+                blk = rx[d].astype(F32)
+                for t in range(tiles):
+                    piece = pad_rows(blk[out_rows * t:out_rows * (t + 1)], out_pad)
+                    xb[out_pad * d:out_pad * (d + 1), LANE * t:LANE * (t + 1)] = piece.astype(BF16)
         else:
             for t in range(tiles):
                 got = lane_swap([rx[groups * t + p].astype(F32) for p in range(groups)])
@@ -372,8 +369,10 @@
             for t in range(tiles):
                 tx[:, attn_rows * t:attn_rows * (t + 1), :] = xb[:, LANE * t:LANE * (t + 1)].reshape(n, attn_rows, LANE)
         elif kind == "out":
-            for t in range(tiles):
-                tx[:, out_pad * t:out_pad * (t + 1), :] = xb[:n * out_pad, LANE * t:LANE * (t + 1)].reshape(n, out_pad, LANE)
+            for d in range(n):
+                blk = xb[out_pad * d:out_pad * (d + 1), :].astype(F32)
+                parts = [blk[:out_rows, LANE * t:LANE * (t + 1)] for t in range(tiles)]
+                tx[d] = pad_rows(jnp.concatenate(parts, axis=0), small_blk).astype(BF16)
         else:
             for t in range(tiles):
                 cols = slice(LANE * t, LANE * (t + 1))
@@ -451,9 +450,7 @@
         else:
             for m, where, _ in mat_rows(i):
                 o = rxo[i][m].astype(F32)
-                if w["kind"] == "out":
-                    o = jnp.concatenate([o[out_pad * t:out_pad * t + out_rows] for t in range(tiles)], axis=0)
-                update(where, o)
+                update(where, o[:out_blk] if w["kind"] == "out" else o)
         sl = pl.ds(w["row0"], w["rows"])
         ag[z, c, sl, :] = wp[sl, :].astype(BF16)
 
@@ -708,7 +705,7 @@
         out_shape += [sds((c_attn, nz, 2, attn_rows, wide), BF16)]
         out_shape += [sds((k, narrow, wide), BF16) for k in counts[1:]]
         w_cnt = (c_attn, mats_b, c_in - mats_b, c_out)
-        w_blk = (attn_blk, small_blk, small_blk, out_pad * tiles)
+        w_blk = (attn_blk, small_blk, small_blk, small_blk)
         dma = lambda *shape: pltpu.SemaphoreType.DMA(shape)
         vm = pltpu.VMEM
         scratch = [

time: 173 us -> 161 us (0.931)
  Pallas kernels: 172 us -> 160 us
    pallas_call x2, Pallas kernels: 172 us -> 160 us  [local_step(): outs = list(hand_over(out_shape)(*call(*grads, *moms, *masters)))]
where the time goes in v6:
time: 161 us
  Pallas kernels  160 us (99%)
    pallas_call x2, Pallas kernels, local_step(): outs = list(hand_over(out_shape)(*call(*grads, *moms, *masters)))  160 us

profile of v6, /device:TPU:21, one launch (start us, length us, event | category | flops | bytes accessed | tf_op | source)
XLA Modules:
  0.0 160.7 jit_solution(3156113045477049705)
XLA Ops:
  0.7 152.8 %muon_step.1 = (f32[4,32,512]{2,1,0:T(8,128)}, f32[2,32,176]{2,1,0:T(8,128)}, f32[11,1,512]{2,1,0:T(1,128)}, f32[16,32,176]{2,1,0:T(8,128)}, f32[11,8,512]{2,1,0...) custom-call(f32[4,8,2,32,512]{4,3,2,1,0:T(8,128)} %bitcast.21, ...), custom_call_target="tpu_custom_call" | custom-call | tf_op jit(solution)/shard_map/muon_step/pallas_call | solution.py:748
  153.4 7.1 %hand_over.1 = (f32[4,32,512]{2,1,0:T(8,128)}, f32[2,32,176]{2,1,0:T(8,128)}, f32[11,1,512]{2,1,0:T(1,128)}, f32[16,32,176]{2,1,0:T(8,128)}, f32[11,8,512]{2,1,0...) custom-call(f32[4,32,512]{2,1,0:T(8,128)} %get-tuple-element.45.refs, ...), custom_call_target="tpu_custom_call" | custom-call | tf_op jit(solution)/shard_map/hand_over/pallas_call | solution.py:748

commit v7 on v6

--- a/solution.py
+++ b/solution.py
@@ -17,25 +17,25 @@
 COEF_C = 2.0315
 
 SCHEDULE = (
-    ("pack", 0), ("rs", 0, 0, 1), ("rs", 0, 1, 1), ("pack", 1), ("rs", 1, 1, 1), ("rs", 1, 0, 1), ("rs", 0, 0, 2),
-    ("rs", 1, 1, 2), ("rs", 0, 1, 2), ("pack", 2), ("rs", 1, 0, 2), ("rs", 0, 0, 3), ("rs", 1, 0, 3),
-    ("rs", 1, 1, 3), ("nat", 0), ("rs", 0, 0, 4), ("rs", 0, 1, 3), ("pack", 3), ("rs", 1, 1, 4), ("rs", 1, 0, 4),
-    ("rs", 3, 1, 1), ("rs", 3, 0, 1), ("rs", 0, 1, 4), ("fin", 1), ("rs", 2, 0, 1), ("rs", 3, 1, 2), ("fin", 0),
-    ("rs", 2, 1, 1), ("rs", 2, 0, 2), ("rs", 3, 0, 2), ("x", 0), ("x", 1), ("rs", 3, 0, 3), ("rs", 2, 0, 3),
-    ("nat", 1), ("rs", 3, 1, 3), ("rs", 2, 1, 2), ("rs", 3, 0, 4), ("own", 0, 1), ("own", 0, 2), ("rs", 2, 0, 4),
-    ("own", 0, 3), ("own", 1, 0), ("rs", 2, 1, 3), ("rs", 3, 1, 4), ("rs", 2, 1, 4), ("mas", 1), ("ag", 1, 0, 1),
-    ("fin", 3), ("fin", 2), ("mas", 0), ("ag", 1, 1, 1), ("ag", 0, 1, 1), ("ag", 1, 0, 2), ("ag", 1, 1, 2),
-    ("x", 2), ("x", 3), ("ag", 0, 1, 2), ("ag", 1, 1, 3), ("ag", 0, 0, 1), ("own", 2, 0), ("ag", 1, 0, 3),
-    ("own", 3, 0), ("ag", 0, 0, 2), ("natout", 0), ("ag", 1, 1, 4), ("ag", 0, 1, 3), ("ag", 1, 0, 4), ("mas", 2),
-    ("ag", 2, 0, 1), ("ag", 2, 1, 1), ("mas", 3), ("ag", 3, 0, 1), ("ag", 1, 1, 5), ("ag", 3, 1, 1),
-    ("ag", 2, 0, 2), ("ag", 2, 1, 2), ("ag", 3, 0, 2), ("natout", 1), ("ag", 3, 1, 2), ("ag", 0, 1, 4),
-    ("ag", 1, 0, 5), ("ag", 2, 1, 3), ("ag", 0, 0, 3), ("ag", 2, 0, 3), ("un", 1), ("ag", 3, 1, 3),
-    ("ag", 0, 1, 5), ("ag", 3, 0, 3), ("ag", 2, 1, 4), ("ag", 2, 0, 4), ("ag", 0, 0, 4), ("ag", 3, 1, 4),
-    ("ag", 3, 0, 4), ("ag", 2, 0, 5), ("ag", 2, 1, 5), ("ag", 0, 0, 5), ("ag", 3, 1, 5), ("ag", 3, 0, 5),
-    ("un", 2), ("un", 3), ("un", 0),
+    ("pack", 0), ("nat", 0), ("rs", 0, 1, 1), ("pack", 1), ("rs", 0, 0, 1), ("rs", 1, 1, 1), ("rs", 0, 1, 2),
+    ("pack", 2), ("rs", 1, 0, 1), ("rs", 0, 0, 2), ("rs", 0, 1, 3), ("rs", 1, 1, 2), ("rs", 1, 0, 2),
+    ("rs", 0, 0, 3), ("rs", 1, 1, 3), ("rs", 1, 0, 3), ("rs", 0, 0, 4), ("rs", 1, 1, 4), ("rs", 0, 1, 4),
+    ("pack", 3), ("rs", 2, 0, 1), ("rs", 1, 0, 4), ("rs", 3, 0, 1), ("rs", 2, 1, 1), ("fin", 1), ("fin", 0),
+    ("rs", 3, 0, 2), ("rs", 2, 1, 2), ("rs", 3, 1, 1), ("x", 0), ("rs", 2, 0, 2), ("rs", 2, 1, 3), ("x", 1),
+    ("rs", 3, 1, 2), ("nat", 1), ("own", 0, 1), ("own", 0, 2), ("rs", 3, 0, 3), ("rs", 2, 0, 3), ("own", 0, 3),
+    ("rs", 3, 1, 3), ("own", 1, 0), ("rs", 2, 1, 4), ("rs", 3, 1, 4), ("rs", 2, 0, 4), ("rs", 3, 0, 4), ("fin", 2),
+    ("mas", 1), ("ag", 1, 1, 1), ("fin", 3), ("mas", 0), ("ag", 0, 1, 1), ("ag", 1, 0, 1), ("ag", 1, 1, 2),
+    ("ag", 0, 0, 1), ("x", 2), ("x", 3), ("ag", 0, 1, 2), ("ag", 1, 1, 3), ("ag", 1, 0, 2), ("own", 2, 0),
+    ("ag", 0, 0, 2), ("own", 3, 0), ("ag", 1, 0, 3), ("ag", 1, 1, 4), ("ag", 0, 1, 3), ("ag", 0, 0, 3), ("mas", 2),
+    ("ag", 2, 0, 1), ("mas", 3), ("ag", 3, 1, 1), ("ag", 1, 1, 5), ("ag", 3, 0, 1), ("ag", 2, 1, 1),
+    ("ag", 1, 0, 4), ("natout", 0), ("ag", 2, 0, 2), ("ag", 3, 1, 2), ("ag", 3, 0, 2), ("ag", 0, 1, 4),
+    ("ag", 1, 0, 5), ("ag", 2, 1, 2), ("natout", 1), ("ag", 2, 0, 3), ("ag", 3, 1, 3), ("ag", 3, 0, 3), ("un", 1),
+    ("ag", 2, 1, 3), ("ag", 3, 1, 4), ("ag", 3, 0, 4), ("ag", 0, 1, 5), ("ag", 0, 0, 4), ("ag", 2, 0, 4),
+    ("ag", 2, 1, 4), ("ag", 3, 0, 5), ("ag", 3, 1, 5), ("ag", 0, 0, 5), ("ag", 2, 0, 5), ("ag", 2, 1, 5),
+    ("un", 3), ("un", 0), ("un", 2),
 )
 
-FIRST_PART = 0.5
+FIRST_PART = 0.4
 
 F32 = jnp.float32
 BF16 = jnp.bfloat16

time: 161 us -> 162 us (level)
  no operation moved by 1% of the time
where the time goes in v7:
time: 162 us
  Pallas kernels  161 us (99%)
    pallas_call x2, Pallas kernels, local_step(): outs = list(hand_over(out_shape)(*call(*grads, *moms, *masters)))  161 us

profile of v7, /device:TPU:21, one launch (start us, length us, event | category | flops | bytes accessed | tf_op | source)
XLA Modules:
  0.0 162.2 jit_solution(3834303016962854412)
XLA Ops:
  0.7 154.3 %muon_step.1 = (f32[4,32,512]{2,1,0:T(8,128)}, f32[2,32,176]{2,1,0:T(8,128)}, f32[11,1,512]{2,1,0:T(1,128)}, f32[16,32,176]{2,1,0:T(8,128)}, f32[11,8,512]{2,1,0...) custom-call(f32[4,8,2,32,512]{4,3,2,1,0:T(8,128)} %bitcast.21, ...), custom_call_target="tpu_custom_call" | custom-call | tf_op jit(solution)/shard_map/muon_step/pallas_call | solution.py:748
  155.0 7.1 %hand_over.1 = (f32[4,32,512]{2,1,0:T(8,128)}, f32[2,32,176]{2,1,0:T(8,128)}, f32[11,1,512]{2,1,0:T(1,128)}, f32[16,32,176]{2,1,0:T(8,128)}, f32[11,8,512]{2,1,0...) custom-call(f32[4,32,512]{2,1,0:T(8,128)} %get-tuple-element.45.refs, ...), custom_call_target="tpu_custom_call" | custom-call | tf_op jit(solution)/shard_map/hand_over/pallas_call | solution.py:748

commit v8 on v6

--- a/solution.py
+++ b/solution.py
@@ -1,5 +1,6 @@
 import functools
 import math
+import types
 import jax
 import jax.numpy as jnp
 from jax import lax
@@ -48,7 +49,7 @@
     return (value + step - 1) // step * step
 
 
-def fused_step(n, counts, attn_rows, wide, narrow, *refs):
+def plan(n, counts, attn_rows, wide, narrow):
     c_attn, c_si, c_so, c_ei, c_eo = counts
     c_in, c_out = c_si + c_ei, c_so + c_eo
     nz = n // 2
@@ -62,19 +63,6 @@
     out_blk = tiles * out_rows
     small_blk = round_up(out_blk, 16)
     cuts = [(q * small_blk, min(small_blk, narrow - q * small_blk)) for q in range(groups)]
-
-    it = iter(refs)
-    take = lambda k: [next(it) for _ in range(k)]
-    g_attn, g_si, g_so, g_ei, g_eo = take(5)
-    m_in = take(5)
-    w_in = take(5)
-    m_out = take(5)
-    w_out = take(5)
-    p_attn, p_si, p_so, p_ei, p_eo = take(5)
-    (gp, rx0, rxr, ag, mp, wp, nat_m, nat_w, nrm, xtx, rxx, otx, rxo, xb, ab, bb,
-     raw_in, raw_out, stage_in, stage_out) = take(20)
-    (s_load, s_nat, s_d2d, s_rs, r_rs, s_nrm, r_nrm, s_x, r_x, s_o, r_o, s_ag, r_ag, s_agd, r_agd, s_out) = take(16)
-
     quad = narrow
     n_quads = c_ei // groups
     quads_b = n_quads // 2
@@ -94,6 +82,55 @@
         w["halves"] = (pl.ds(w["row0"], split), pl.ds(w["row0"] + split, w["rows"] - split))
         w["quad0"] = w["row0"] + w.get("shared", 0) * small_blk
     out0 = waves[3]["row0"]
+    cut_in, cut_out = groups * quads_b, c_eo // groups
+    return types.SimpleNamespace(**locals())
+
+
+def lane_swap(blocks):
+    groups, in_rows = len(blocks), LANE // len(blocks)
+    lane = lax.broadcasted_iota(jnp.int32, (1, LANE), 1)
+    blocks = list(blocks)
+    dist = groups // 2
+    while dist:
+        width = dist * in_rows
+        low = lax.rem(lane // width, 2) == 0
+        for q in range(groups):
+            if (q // dist) % 2 == 0:
+                x, y = blocks[q], blocks[q + dist]
+                if 2 * width == LANE:
+                    turned = pltpu.roll(jnp.where(low, y, x), width, axis=1)
+                    blocks[q] = jnp.where(low, x, turned)
+                    blocks[q + dist] = jnp.where(low, turned, y)
+                else:
+                    blocks[q] = jnp.where(low, x, pltpu.roll(y, width, axis=1))
+                    blocks[q + dist] = jnp.where(low, pltpu.roll(x, LANE - width, axis=1), y)
+        dist //= 2
+    return blocks
+
+def pad_rows(x, rows):
+    if x.shape[0] == rows:
+        return x
+    return jnp.concatenate([x, jnp.zeros((rows - x.shape[0], x.shape[1]), x.dtype)], axis=0)
+
+
+def fused_step(n, counts, attn_rows, wide, narrow, *refs):
+    g = plan(n, counts, attn_rows, wide, narrow)
+    c_attn, c_si, c_so, c_ei, c_eo, c_in, c_out = g.c_attn, g.c_si, g.c_so, g.c_ei, g.c_eo, g.c_in, g.c_out
+    nz, hops_far, hops_near, tiles, in_rows, groups, out_rows = g.nz, g.hops_far, g.hops_near, g.tiles, g.in_rows, g.groups, g.out_rows
+    out_pad, attn_blk, out_blk, small_blk, cuts, quad, n_quads = g.out_pad, g.attn_blk, g.out_blk, g.small_blk, g.cuts, g.quad, g.n_quads
+    quads_b, rows_d, waves, n_waves, out0, cut_in, cut_out = g.quads_b, g.rows_d, g.waves, g.n_waves, g.out0, g.cut_in, g.cut_out
+
+    it = iter(refs)
+    take = lambda k: [next(it) for _ in range(k)]
+    g_attn, g_si, g_so, g_ei, g_eo = take(5)
+    m_in = take(5)
+    w_in = take(5)
+    m_out = take(5)
+    w_out = take(5)
+    p_raw, = take(1)
+    (gp, rx0, rxr, ag, mp, wp, nat_m, nat_w, nrm, xtx, rxx, otx, rxo, xb, ab, bb,
+     raw_in, raw_out) = take(18)
+    (s_load, s_nat, s_d2d, s_rs, r_rs, s_nrm, r_nrm, s_x, r_x, s_o, r_o, s_ag, r_ag, s_agd, r_agd, s_out) = take(16)
 
     me = lax.axis_index("data")
     z = me // 2
@@ -115,32 +152,6 @@
         return [pltpu.make_async_copy(srcs[k], dsts[k], s_nat.at[which, k])
                 for which, (srcs, dsts) in enumerate(((m_in, nat_m), (w_in, nat_w))) for k in range(5)]
 
-    def lane_swap(blocks):
-        lane = lax.broadcasted_iota(jnp.int32, (1, LANE), 1)
-        blocks = list(blocks)
-        dist = groups // 2
-        while dist:
-            width = dist * in_rows
-            low = lax.rem(lane // width, 2) == 0
-            for q in range(groups):
-                if (q // dist) % 2 == 0:
-                    x, y = blocks[q], blocks[q + dist]
-                    if 2 * width == LANE:
-                        turned = pltpu.roll(jnp.where(low, y, x), width, axis=1)
-                        blocks[q] = jnp.where(low, x, turned)
-                        blocks[q + dist] = jnp.where(low, turned, y)
-                    else:
-                        blocks[q] = jnp.where(low, x, pltpu.roll(y, width, axis=1))
-                        blocks[q + dist] = jnp.where(low, pltpu.roll(x, LANE - width, axis=1), y)
-            dist //= 2
-        return blocks
-
-    def pad_rows(x, rows):
-        if x.shape[0] == rows:
-            return x
-        return jnp.concatenate([x, jnp.zeros((rows - x.shape[0], x.shape[1]), x.dtype)], axis=0)
-
-    cut_in, cut_out = groups * quads_b, c_eo // groups
 
     def loads():
         return [
@@ -547,64 +558,8 @@
         for h in range(2):
             for key in range(nz):
                 agd[i, h, key].wait_recv()
-        if w["kind"] == "attn":
-            for m in range(c_attn):
-                for t in range(tiles):
-                    out_copies.append(pltpu.make_async_copy(
-                        ag.at[:, :, pl.ds(m * attn_blk + t * attn_rows, attn_rows), :],
-                        p_attn.at[m, :, :, :, pl.ds(LANE * t, LANE)], s_out.at[10 + m * tiles + t]))
-                    out_copies[-1].start()
-        elif w["kind"] == "in":
-            for j in range(w["shared"]):
-                sl = pl.ds(w["row0"] + small_blk * j, small_blk)
-                for t in range(tiles):
-                    devs = [groups * t + p for p in range(groups)]
-                    got = lane_swap([ag[d // 2, d % 2, sl, :].astype(F32) for d in devs])
-                    for q, (r, k) in enumerate(cuts):
-                        stage_in[j, r:r + k, LANE * t:LANE * (t + 1)] = got[q][:k].astype(BF16)
-
-            def body(j, carry):
-                off = pl.multiple_of(w["quad0"] + quad * j, 16)
-                first = c_si + groups * (w["first"] + j)
-                for t in range(tiles):
-                    devs = [groups * t + p for p in range(groups)]
-                    got = lane_swap([ag[d // 2, d % 2, pl.ds(off, quad), :].astype(F32) for d in devs])
-                    for p in range(groups):
-                        stage_in[first + p, :, LANE * t:LANE * (t + 1)] = got[p].astype(BF16)
-                return carry
-
-            lax.fori_loop(0, w["quads"], body, 0)
-            k = 10 + c_attn * tiles
-            if w["shared"]:
-                out_copy(stage_in.at[pl.ds(0, c_si)], p_si, k)
-            first, cnt = groups * w["first"], groups * w["quads"]
-            out_copy(stage_in.at[pl.ds(c_si + first, cnt)], p_ei.at[pl.ds(first, cnt)], k + 1 + (w["first"] > 0))
-        else:
-            def put(blk, m, first, d):
-                for t in range(tiles):
-                    r = out_blk * m + t * out_rows
-                    raw_out[first + m, out_rows * d:out_rows * (d + 1), LANE * t:LANE * (t + 1)] = blk[r:r + out_rows]
-
-            def body(j, carry):
-                off = pl.multiple_of(out0 + groups * out_blk * j, 16)
-                for d in range(n):
-                    blk = ag[d // 2, d % 2, pl.ds(off, groups * out_blk), :].astype(F32)
-                    for p in range(groups):
-                        put(blk, p, groups * j, d)
-                for p in range(groups):
-                    stage_out[groups * j + p] = raw_out[groups * j + p].astype(BF16)
-                return carry
-
-            lax.fori_loop(0, cut_out, body, 0)
-            for d in range(n):
-                blk = ag[d // 2, d % 2, pl.ds(out0 + c_eo * out_blk, rows_d - c_eo * out_blk), :].astype(F32)
-                for m in range(c_so):
-                    put(blk, m, c_eo, d)
-            for m in range(c_eo, c_out):
-                stage_out[m] = raw_out[m].astype(BF16)
-            k = 13 + c_attn * tiles
-            out_copy(stage_out.at[pl.ds(c_eo, c_so)], p_so, k)
-            out_copy(stage_out.at[pl.ds(0, c_eo)], p_eo, k + 1)
+        sl = pl.ds(w["row0"], w["rows"])
+        out_copy(ag.at[:, :, sl, :], p_raw.at[:, :, sl, :], 10 + i)
 
     def both(func, length, i, h, s):
         for dr in range(2):
@@ -643,33 +598,109 @@
             pltpu.make_async_copy(view, view, s_o.at[i]).wait()
 
 
-def hand_over(shapes):
-    count = len(shapes)
-    pieces = []
-    for k, x in enumerate(shapes):
-        parts = next((p for p in (4, 2) if x.shape[0] % p == 0 and x.size > 400000), 1)
-        step = x.shape[0] // parts
-        pieces += [(k, p * step, step) for p in range(parts)]
+def hand_over(g, shapes, params, raw):
+    n, count = g.n, len(shapes)
+    c_attn, c_si, c_so, c_ei, c_eo = g.counts
+    nz, tiles, groups, cuts, attn_rows, attn_blk, out_rows, out_blk = (
+        g.nz, g.tiles, g.groups, g.cuts, g.attn_rows, g.attn_blk, g.out_rows, g.out_blk)
+    small_blk, quad, out0, rows_d, cut_out, c_in, c_out = g.small_blk, g.quad, g.out0, g.rows_d, g.cut_out, g.c_in, g.c_out
+    n_out = count + c_attn * tiles + 5
 
     def kernel(*refs):
-        src, dst, buf, sem_in, sem_out = refs[:count], refs[count:2 * count], refs[2 * count:3 * count], refs[-2], refs[-1]
-        first = [pltpu.make_async_copy(src[k].at[pl.ds(r, m)], buf[k].at[pl.ds(r, m)], sem_in.at[i])
-                 for i, (k, r, m) in enumerate(pieces)]
-        second = [pltpu.make_async_copy(buf[k].at[pl.ds(r, m)], dst[k].at[pl.ds(r, m)], sem_out.at[i])
-                  for i, (k, r, m) in enumerate(pieces)]
-        for cp in first:
+        src, raw_ref = refs[:count], refs[count]
+        dst = refs[count + 1:2 * count + 1]
+        p_attn, p_si, p_so, p_ei, p_eo = refs[2 * count + 1:2 * count + 6]
+        bufs = refs[2 * count + 6:3 * count + 6]
+        ag, raw_out, stage_in, stage_out, s_in, s_out = refs[3 * count + 6:]
+        out_copies = []
+
+        def out_copy(a, b, k):
+            out_copies.append(pltpu.make_async_copy(a, b, s_out.at[k]))
+            out_copies[-1].start()
+
+        first = []
+        for i in (1, 2, 3, 0):
+            sl = pl.ds(g.waves[i]["row0"], g.waves[i]["rows"])
+            first.append((i, pltpu.make_async_copy(raw_ref.at[:, :, sl, :], ag.at[:, :, sl, :], s_in.at[count + i])))
+            first[-1][1].start()
+        plain = [pltpu.make_async_copy(src[k], bufs[k], s_in.at[k]) for k in range(count)]
+        for cp in plain:
             cp.start()
-        for one, two in zip(first, second):
-            one.wait()
-            two.start()
-        for cp in second:
+        for i, cp in first:
+            w = g.waves[i]
             cp.wait()
+            if w["kind"] == "attn":
+                for m in range(c_attn):
+                    for t in range(tiles):
+                        out_copies.append(pltpu.make_async_copy(
+                            ag.at[:, :, pl.ds(m * attn_blk + t * attn_rows, attn_rows), :],
+                            p_attn.at[m, :, :, :, pl.ds(LANE * t, LANE)], s_out.at[len(shapes) + m * tiles + t]))
+                        out_copies[-1].start()
+            elif w["kind"] == "in":
+                for j in range(w["shared"]):
+                    sl = pl.ds(w["row0"] + small_blk * j, small_blk)
+                    for t in range(tiles):
+                        devs = [groups * t + p for p in range(groups)]
+                        got = lane_swap([ag[d // 2, d % 2, sl, :].astype(F32) for d in devs])
+                        for q, (r, k) in enumerate(cuts):
+                            stage_in[j, r:r + k, LANE * t:LANE * (t + 1)] = got[q][:k].astype(BF16)
+
+                def body(j, carry):
+                    off = pl.multiple_of(w["quad0"] + quad * j, 16)
+                    first = c_si + groups * (w["first"] + j)
+                    for t in range(tiles):
+                        devs = [groups * t + p for p in range(groups)]
+                        got = lane_swap([ag[d // 2, d % 2, pl.ds(off, quad), :].astype(F32) for d in devs])
+                        for p in range(groups):
+                            stage_in[first + p, :, LANE * t:LANE * (t + 1)] = got[p].astype(BF16)
+                    return carry
+
+                lax.fori_loop(0, w["quads"], body, 0)
+                k = len(shapes) + c_attn * tiles
+                if w["shared"]:
+                    out_copy(stage_in.at[pl.ds(0, c_si)], p_si, k)
+                first, cnt = groups * w["first"], groups * w["quads"]
+                out_copy(stage_in.at[pl.ds(c_si + first, cnt)], p_ei.at[pl.ds(first, cnt)], k + 1 + (w["first"] > 0))
+            else:
+                def put(blk, m, first, d):
+                    for t in range(tiles):
+                        r = out_blk * m + t * out_rows
+                        raw_out[first + m, out_rows * d:out_rows * (d + 1), LANE * t:LANE * (t + 1)] = blk[r:r + out_rows]
+
+                def body(j, carry):
+                    off = pl.multiple_of(out0 + groups * out_blk * j, 16)
+                    for d in range(n):
+                        blk = ag[d // 2, d % 2, pl.ds(off, groups * out_blk), :].astype(F32)
+                        for p in range(groups):
+                            put(blk, p, groups * j, d)
+                    for p in range(groups):
+                        stage_out[groups * j + p] = raw_out[groups * j + p].astype(BF16)
+                    return carry
+
+                lax.fori_loop(0, cut_out, body, 0)
+                for d in range(n):
+                    blk = ag[d // 2, d % 2, pl.ds(out0 + c_eo * out_blk, rows_d - c_eo * out_blk), :].astype(F32)
+                    for m in range(c_so):
+                        put(blk, m, c_eo, d)
+                for m in range(c_eo, c_out):
+                    stage_out[m] = raw_out[m].astype(BF16)
+                k = len(shapes) + 3 + c_attn * tiles
+                out_copy(stage_out.at[pl.ds(c_eo, c_so)], p_so, k)
+                out_copy(stage_out.at[pl.ds(0, c_eo)], p_eo, k + 1)
+        for k in range(count):
+            plain[k].wait()
+            out_copy(bufs[k], dst[k], k)
+        for cp in out_copies:
+            cp.wait()
 
     any_spec = pl.BlockSpec(memory_space=pl.ANY)
+    vm = pltpu.VMEM
     return pl.pallas_call(
-        kernel, out_shape=shapes, in_specs=[any_spec] * count, out_specs=[any_spec] * count,
-        scratch_shapes=[pltpu.VMEM(x.shape, x.dtype) for x in shapes]
-        + [pltpu.SemaphoreType.DMA((len(pieces),)), pltpu.SemaphoreType.DMA((len(pieces),))],
+        kernel, out_shape=shapes + params, in_specs=[any_spec] * (count + 1), out_specs=[any_spec] * (count + len(params)),
+        scratch_shapes=[vm(x.shape, x.dtype) for x in shapes]
+        + [vm(raw.shape, BF16), vm((c_out, g.narrow, g.wide), F32), vm((c_in, g.narrow, g.wide), BF16),
+           vm((c_out, g.narrow, g.wide), BF16)]
+        + [pltpu.SemaphoreType.DMA((count + 4,)), pltpu.SemaphoreType.DMA((n_out,))],
         name="hand_over")
 
 
@@ -702,8 +733,8 @@
 
         sds = jax.ShapeDtypeStruct
         out_shape = [sds(m.shape, F32) for m in moms] * 2
-        out_shape += [sds((c_attn, nz, 2, attn_rows, wide), BF16)]
-        out_shape += [sds((k, narrow, wide), BF16) for k in counts[1:]]
+        params = [sds((c_attn, nz, 2, attn_rows, wide), BF16)] + [sds((k, narrow, wide), BF16) for k in counts[1:]]
+        raw = sds((nz, 2, rows, LANE), BF16)
         w_cnt = (c_attn, mats_b, c_in - mats_b, c_out)
         w_blk = (attn_blk, small_blk, small_blk, small_blk)
         dma = lambda *shape: pltpu.SemaphoreType.DMA(shape)
@@ -727,25 +758,23 @@
             vm((n * attn_rows, n * attn_rows), BF16),
             vm((c_in, narrow, wide), F32),
             vm((c_out, narrow, wide), F32),
-            vm((c_in, narrow, wide), BF16),
-            vm((c_out, narrow, wide), BF16),
             dma(6), dma(2, 5), dma(2, 4, nz), dma(4, 4, hops), dma(4, 4, hops),
             dma(4), dma(4), dma(4, max(w_cnt)), dma(4), dma(4), dma(4),
             dma(4, 4, hops), dma(4, 4, hops), dma(4, 2, nz), dma(4, 2, nz),
-            dma(15 + c_attn * tiles),
+            dma(14),
         ]
         any_spec = pl.BlockSpec(memory_space=pl.ANY)
         call = pl.pallas_call(
             functools.partial(fused_step, n, counts, attn_rows, wide, narrow),
-            out_shape=out_shape,
+            out_shape=out_shape + [raw],
             in_specs=[any_spec] * 15,
-            out_specs=[any_spec] * 15,
+            out_specs=[any_spec] * 11,
             scratch_shapes=scratch,
             compiler_params=pltpu.CompilerParams(
                 collective_id=0, has_side_effects=True, vmem_limit_bytes=67043328),
             name="muon_step",
         )
-        outs = list(hand_over(out_shape)(*call(*grads, *moms, *masters)))
+        outs = list(hand_over(plan(n, counts, attn_rows, wide, narrow), out_shape, params, raw)(*call(*grads, *moms, *masters)))
         outs[:5], outs[5:10] = flip(outs[:5]), flip(outs[5:10])
         outs[10] = outs[10].reshape(c_attn, n * attn_rows, wide)
         outs[11], outs[13] = turn(outs[11]), turn(outs[13])

time: 161 us -> 160 us (level)
  no operation moved by 1% of the time
where the time goes in v8:
time: 160 us
  Pallas kernels  159 us (99%)
    pallas_call x1, Pallas kernels, local_step(): call(*grads, *moms, *masters)  152 us
    pallas_call x1, Pallas kernels, local_step(): hand_over(plan(n, counts, attn_rows, wide, narrow), out_shape, params, raw)  7.57 us

profile of v8, /device:TPU:21, one launch (start us, length us, event | category | flops | bytes accessed | tf_op | source)
XLA Modules:
  0.0 160.3 jit_solution(5396142220072979040)
XLA Ops:
  0.7 151.9 %muon_step.1 = (f32[4,32,512]{2,1,0:T(8,128)}, f32[2,32,176]{2,1,0:T(8,128)}, f32[11,1,512]{2,1,0:T(1,128)}, f32[16,32,176]{2,1,0:T(8,128)}, f32[11,8,512]{2,1,0...) custom-call(f32[4,8,2,32,512]{4,3,2,1,0:T(8,128)} %bitcast.21, ...), custom_call_target="tpu_custom_call" | custom-call | tf_op jit(solution)/shard_map/muon_step/pallas_call | solution.py:777
  152.5 7.6 %hand_over.1 = (f32[4,32,512]{2,1,0:T(8,128)}, f32[2,32,176]{2,1,0:T(8,128)}, f32[11,1,512]{2,1,0:T(1,128)}, f32[16,32,176]{2,1,0:T(8,128)}, f32[11,8,512]{2,1,0...) custom-call(f32[4,32,512]{2,1,0:T(8,128)} %get-tuple-element.41.refs, ...), custom_call_target="tpu_custom_call" | custom-call | tf_op jit(solution)/shard_map/hand_over/pallas_call | solution.py:777

commit v9 on v8

--- a/solution.py
+++ b/solution.py
@@ -18,22 +18,22 @@
 COEF_C = 2.0315
 
 SCHEDULE = (
-    ("pack", 0), ("rs", 0, 0, 1), ("rs", 0, 1, 1), ("pack", 1), ("rs", 1, 1, 1), ("rs", 1, 0, 1), ("rs", 0, 0, 2),
-    ("rs", 1, 1, 2), ("rs", 0, 1, 2), ("pack", 2), ("rs", 1, 0, 2), ("rs", 0, 0, 3), ("rs", 1, 0, 3),
-    ("rs", 1, 1, 3), ("nat", 0), ("rs", 0, 0, 4), ("rs", 0, 1, 3), ("pack", 3), ("rs", 1, 1, 4), ("rs", 1, 0, 4),
-    ("rs", 3, 1, 1), ("rs", 3, 0, 1), ("rs", 0, 1, 4), ("fin", 1), ("rs", 2, 0, 1), ("rs", 3, 1, 2), ("fin", 0),
-    ("rs", 2, 1, 1), ("rs", 2, 0, 2), ("rs", 3, 0, 2), ("x", 0), ("x", 1), ("rs", 3, 0, 3), ("rs", 2, 0, 3),
-    ("nat", 1), ("rs", 3, 1, 3), ("rs", 2, 1, 2), ("rs", 3, 0, 4), ("own", 0, 1), ("own", 0, 2), ("rs", 2, 0, 4),
-    ("own", 0, 3), ("own", 1, 0), ("rs", 2, 1, 3), ("rs", 3, 1, 4), ("rs", 2, 1, 4), ("mas", 1), ("ag", 1, 0, 1),
-    ("fin", 3), ("fin", 2), ("mas", 0), ("ag", 1, 1, 1), ("ag", 0, 1, 1), ("ag", 1, 0, 2), ("ag", 1, 1, 2),
-    ("x", 2), ("x", 3), ("ag", 0, 1, 2), ("ag", 1, 1, 3), ("ag", 0, 0, 1), ("own", 2, 0), ("ag", 1, 0, 3),
-    ("own", 3, 0), ("ag", 0, 0, 2), ("natout", 0), ("ag", 1, 1, 4), ("ag", 0, 1, 3), ("ag", 1, 0, 4), ("mas", 2),
-    ("ag", 2, 0, 1), ("ag", 2, 1, 1), ("mas", 3), ("ag", 3, 0, 1), ("ag", 1, 1, 5), ("ag", 3, 1, 1),
-    ("ag", 2, 0, 2), ("ag", 2, 1, 2), ("ag", 3, 0, 2), ("natout", 1), ("ag", 3, 1, 2), ("ag", 0, 1, 4),
-    ("ag", 1, 0, 5), ("ag", 2, 1, 3), ("ag", 0, 0, 3), ("ag", 2, 0, 3), ("un", 1), ("ag", 3, 1, 3),
-    ("ag", 0, 1, 5), ("ag", 3, 0, 3), ("ag", 2, 1, 4), ("ag", 2, 0, 4), ("ag", 0, 0, 4), ("ag", 3, 1, 4),
-    ("ag", 3, 0, 4), ("ag", 2, 0, 5), ("ag", 2, 1, 5), ("ag", 0, 0, 5), ("ag", 3, 1, 5), ("ag", 3, 0, 5),
-    ("un", 2), ("un", 3), ("un", 0),
+    ("pack", 0), ("rs", 0, 0, 1), ("rs", 0, 1, 1), ("pack", 1), ("rs", 1, 0, 1), ("rs", 0, 0, 2), ("rs", 0, 1, 2),
+    ("rs", 1, 1, 1), ("rs", 0, 0, 3), ("rs", 1, 0, 2), ("pack", 2), ("nat", 0), ("rs", 1, 1, 2), ("rs", 2, 1, 1),
+    ("rs", 1, 0, 3), ("rs", 1, 1, 3), ("pack", 3), ("rs", 3, 0, 1), ("rs", 1, 0, 4), ("rs", 0, 0, 4),
+    ("rs", 0, 1, 3), ("rs", 2, 1, 2), ("rs", 3, 1, 1), ("rs", 0, 1, 4), ("rs", 2, 0, 1), ("rs", 1, 1, 4),
+    ("fin", 0), ("rs", 3, 0, 2), ("nat", 1), ("rs", 2, 1, 3), ("fin", 1), ("rs", 2, 0, 2), ("x", 0),
+    ("rs", 3, 1, 2), ("rs", 2, 1, 4), ("rs", 2, 0, 3), ("x", 1), ("rs", 3, 0, 3), ("own", 0, 1), ("rs", 3, 1, 3),
+    ("own", 0, 2), ("own", 0, 3), ("rs", 2, 0, 4), ("own", 1, 0), ("rs", 3, 0, 4), ("rs", 3, 1, 4), ("fin", 2),
+    ("mas", 1), ("ag", 1, 1, 1), ("mas", 0), ("ag", 0, 0, 1), ("fin", 3), ("ag", 0, 1, 1), ("ag", 1, 0, 1),
+    ("ag", 0, 0, 2), ("x", 2), ("x", 3), ("ag", 1, 1, 2), ("ag", 1, 0, 2), ("ag", 0, 1, 2), ("ag", 0, 0, 3),
+    ("own", 2, 0), ("own", 3, 0), ("ag", 1, 1, 3), ("ag", 1, 0, 3), ("ag", 0, 1, 3), ("ag", 1, 1, 4),
+    ("ag", 0, 0, 4), ("mas", 2), ("mas", 3), ("ag", 3, 1, 1), ("ag", 2, 1, 1), ("natout", 0), ("ag", 3, 0, 1),
+    ("ag", 2, 0, 1), ("natout", 1), ("ag", 0, 1, 4), ("ag", 3, 1, 2), ("ag", 2, 1, 2), ("ag", 1, 0, 4),
+    ("ag", 0, 0, 5), ("ag", 3, 0, 2), ("ag", 1, 1, 5), ("ag", 2, 0, 2), ("ag", 0, 1, 5), ("ag", 1, 0, 5),
+    ("ag", 3, 1, 3), ("ag", 3, 0, 3), ("ag", 2, 1, 3), ("ag", 2, 0, 3), ("un", 1), ("ag", 3, 1, 4),
+    ("ag", 3, 0, 4), ("ag", 2, 0, 4), ("ag", 2, 1, 4), ("un", 0), ("ag", 3, 1, 5), ("ag", 3, 0, 5),
+    ("ag", 2, 0, 5), ("ag", 2, 1, 5), ("un", 3), ("un", 2),
 )
 
 FIRST_PART = 0.5

time: 160 us -> 159 us (level)
  no operation moved by 1% of the time
where the time goes in v9:
time: 159 us
  Pallas kernels  158 us (99%)
    pallas_call x1, Pallas kernels, local_step(): call(*grads, *moms, *masters)  150 us
    pallas_call x1, Pallas kernels, local_step(): hand_over(plan(n, counts, attn_rows, wide, narrow), out_shape, params, raw)  7.57 us

profile of v9, /device:TPU:21, one launch (start us, length us, event | category | flops | bytes accessed | tf_op | source)
XLA Modules:
  0.0 158.8 jit_solution(17714217282461433343)
XLA Ops:
  0.7 150.4 %muon_step.1 = (f32[4,32,512]{2,1,0:T(8,128)}, f32[2,32,176]{2,1,0:T(8,128)}, f32[11,1,512]{2,1,0:T(1,128)}, f32[16,32,176]{2,1,0:T(8,128)}, f32[11,8,512]{2,1,0...) custom-call(f32[4,8,2,32,512]{4,3,2,1,0:T(8,128)} %bitcast.21, ...), custom_call_target="tpu_custom_call" | custom-call | tf_op jit(solution)/shard_map/muon_step/pallas_call | solution.py:777
  151.1 7.6 %hand_over.1 = (f32[4,32,512]{2,1,0:T(8,128)}, f32[2,32,176]{2,1,0:T(8,128)}, f32[11,1,512]{2,1,0:T(1,128)}, f32[16,32,176]{2,1,0:T(8,128)}, f32[11,8,512]{2,1,0...) custom-call(f32[4,32,512]{2,1,0:T(8,128)} %get-tuple-element.41.refs, ...), custom_call_target="tpu_custom_call" | custom-call | tf_op jit(solution)/shard_map/hand_over/pallas_call | solution.py:777
